TPU v7x, 256 devices: a whole 4x4x8 slice. The times are simulated.
256 devices in a mesh: gz: 32 (over x, z), gy: 8 (over y, core).
Axes of the slice: x: 4, y: 4, z: 8, core: 2. Of those that a mesh axis runs over, the one named last changes fastest.
Arguments:
- ranks: float32 [256, 128, 512], P('gz', 'gy'), may hold values from 1 to 2
- seeds: float32 [3, 256, 128, 512], P(None, 'gz', 'gy'), may hold values from 0.25 to 1
- flags: int32 [256, 128, 512], P('gz', 'gy'), may hold values 0 or 1
Outputs:
- states: int32 [256, 128, 512], P('gz', 'gy')
- undecided: int32 [3], replicated
All inputs are finite; a program needn't handle non-finite values. No bound on the sum of `flags` on one device may be relied on, other than what follows from the above.
Results may differ from a plain program's by a relative error of at most 0.000001.
Values sent between devices are 32-bit elements; how exact they have to be, the bound alone decides.
A program may use at most 64 MiB of HBM per device.

v0:
```python
import functools

import jax
import jax.numpy as jnp
from jax import lax
from jax.sharding import Mesh
from jax.sharding import PartitionSpec as P

ROUNDS = 3
GZ = ("gz_0", "gz_1")
GY = ("gy_0", "gy_1")
GZ_GY = ("gz_0", "gz_1", "gy_0", "gy_1")


def passed_along(value, axis, steps):
    count = lax.axis_size(axis)
    initial, last = (max(0, -steps), min(count, count - steps))
    return lax.ppermute(value, axis, [(source, source + steps) for source in range(initial, last)])


def padded(x, sides, width):
    edges = {}
    for axis, dim in sides:
        count, length = (lax.axis_size(axis), x.shape[dim])
        up = [(i, (i + 1) % count) for i in range(count - 1)]
        last = lax.slice_in_dim(x, length - width, length, axis=dim)
        initial = lax.slice_in_dim(x, 0, width, axis=dim)
        edges[dim] = (
            lax.ppermute(last, axis, up),
            lax.ppermute(initial, axis, [(b, a) for a, b in up]),
        )
    done = []
    for _, dim in sides:
        low, high = edges[dim]
        around = [(width, width) if d in done else (0, 0) for d in range(x.ndim)]
        x = jnp.concatenate([jnp.pad(low, around), x, jnp.pad(high, around)], axis=dim)
        done.append(dim)
    return x


def extended(cells, sides, width):
    for axis, dim in sides:
        count = lax.axis_size(axis)
        ends = count - 1
        head = lax.slice_in_dim(cells, 0, width, axis=dim)
        tail = lax.slice_in_dim(cells, cells.shape[dim] - width, cells.shape[dim], axis=dim)
        cells = jnp.concatenate(
            [
                lax.ppermute(tail, axis, [(i, (i + 1) % count) for i in range(ends)]),
                cells,
                lax.ppermute(head, axis, [((i + 1) % count, i) for i in range(ends)]),
            ],
            axis=dim,
        )
    return cells


def one_axis_at_a_time(x, axes):
    return functools.reduce(lax.psum, axes, x)


def beside_all(ext, fill):
    wide = jnp.pad(ext, ((0, 0), (0, 0), (1, 1)), constant_values=fill)
    return [
        wide[1:-1, 1:-1, 2:],
        wide[1:-1, 1:-1, :-2],
        wide[1:-1, 2:, 1:-1],
        wide[1:-1, :-2, 1:-1],
        wide[2:, 1:-1, 1:-1],
        wide[:-2, 1:-1, 1:-1],
    ]


def bit_of(bits, number):
    return bits // 2**number % 2


def strength(couplings, rowmax, others):
    bits = jnp.zeros(rowmax.shape, jnp.int32)
    scale = jnp.ones(rowmax.shape, jnp.float32)
    for direction in range(6):
        cost = couplings[direction]
        depends = ((cost > 0) & (2.0 * cost >= rowmax)).astype(jnp.int32)
        feeds = ((cost > 0) & (2.0 * cost >= others[direction])).astype(jnp.int32)
        bits = bits + depends * 2**direction + feeds * 2 ** (direction + 6)
        scale = scale * jnp.where(feeds == 1, 2.0, 1.0).astype(jnp.float32)
    return (bits, scale)


def select(packed_ext, bits):
    center = packed_ext[1:-1, 1:-1]
    values = beside_all(packed_ext, -3.0)
    nearest = jnp.full(center.shape, -3.0, center.dtype)
    for direction in range(6):
        linked = bit_of(bits, direction) + bit_of(bits, direction + 6) > 0
        nearest = jnp.maximum(nearest, jnp.where(linked, values[direction], -3.0))
    return ((center >= 0) & (center > nearest)).astype(jnp.int32)


def finer(coarse_ext, bits):
    values = beside_all(coarse_ext, 0)
    hit = jnp.zeros(bits.shape, jnp.int32)
    for direction in range(6):
        hit = hit + bit_of(bits, direction) * values[direction]
    return hit


def per_device(ranks, seeds, flags):
    depth, rows, width = ranks.shape
    zpos = lax.axis_index(GZ) * depth + jnp.arange(depth, dtype=jnp.int32)[:, None, None]
    ypos = lax.axis_index(GY) * rows + jnp.arange(rows, dtype=jnp.int32)[None, :, None]
    xpos = jnp.arange(width, dtype=jnp.int32)[None, None, :]
    total_z = depth * lax.axis_size(GZ)
    total_y = rows * lax.axis_size(GY)
    zero = jnp.zeros((), jnp.float32)
    c0 = jnp.where(xpos < width - 1, seeds[0], zero)
    c2 = jnp.where(ypos < total_y - 1, seeds[1], zero)
    c4 = jnp.where(zpos < total_z - 1, seeds[2], zero)
    c1 = jnp.pad(c0[:, :, :-1], ((0, 0), (0, 0), (1, 0)))
    below_row = passed_along(c2[:, -1:], GY, 1)
    c3 = jnp.concatenate([below_row, c2[:, :-1]], axis=1)
    below_plane = passed_along(c4[-1:], GZ, 1)
    c5 = jnp.concatenate([below_plane, c4[:-1]], axis=0)
    couplings = [c0, c1, c2, c3, c4, c5]
    rowmax = c0
    for item in couplings[1:]:
        rowmax = jnp.maximum(rowmax, item)
    rowmax_ext = padded(rowmax, ((GZ, 0), (GY, 1)), 1)
    others = beside_all(rowmax_ext, 0.0)
    bits, scale = strength(couplings, rowmax, others)
    measure = ranks * scale
    bits_inner = padded(bits, ((GZ, 0), (GY, 1)), 1)
    state = flags
    totals = []
    for step in range(ROUNDS):
        packed = jnp.where(state == 0, measure, jnp.where(state == 2, -2.0, -1.0))
        packed_wide = extended(packed, ((GZ, 0), (GY, 1)), 2)
        coarse_ext = select(packed_wide, bits_inner)
        coarse = coarse_ext[1:-1, 1:-1]
        hit = finer(coarse_ext, bits)
        state = jnp.where(coarse == 1, 2, jnp.where((state == 0) & (hit > 0), 1, state))
        local = jnp.sum((state == 0).astype(jnp.int32))
        totals.append(one_axis_at_a_time(local, GZ_GY))
    undecided = jnp.stack(totals)
    return (state, undecided)


def solution(mesh):
    finer = Mesh(mesh.devices.reshape(4, 8, 4, 2), ("gz_0", "gz_1", "gy_0", "gy_1"))
    placed = (P(GZ, GY, None), P(None, GZ, GY, None), P(GZ, GY, None))
    return jax.shard_map(
        per_device, mesh=finer, in_specs=placed, out_specs=(P(GZ, GY, None), P()), check_vma=False
    )
```

profile of v0, /device:TPU:1, one launch (start us, length us, event | category | flops | bytes accessed | tf_op | source)
XLA Modules:
  0.0 158.0 jit_solution(2309753013258576908)
XLA Ops:
  1.9 4.4 %collective-permute-start.1 = (f32[1,16,512]{2,1,0:T(8,128)S(1)}, f32[1,16,512]{2,1,0:T(8,128)S(1)}, u32[]{:S(2)}, u32[]{:S(2)}) collective-permute-start(f32[1,16,512]{2,1,0:T(8,128)S(1)} %slice.347), channel_id=1, source_target_pairs={{0,8},{8,16},{16,24},{24,32},{32,40},{40,48},{48,56},{56,64},{64,7... | collective-permute-start | bytes 98312 | tf_op jit(solution)/shard_map/ppermute | solution.py:18
  6.3 4.0 %collective-permute-start = (f32[8,1,512]{2,1,0:T(1,128)S(1)}, f32[8,1,512]{2,1,0:T(1,128)S(1)}, u32[]{:S(2)}, u32[]{:S(2)}) collective-permute-start(f32[8,1,512]{2,1,0:T(1,128)S(1)} %slice.345), channel_id=1, source_target_pairs={{0,1},{1,2},{2,3},{3,4},{4,5},{5,6},{6,7},{8,9},{9,10},{10,11},{11... | collective-permute-start | bytes 49160 | tf_op jit(solution)/shard_map/ppermute | solution.py:18
  12.7 4.2 %collective-permute-start.3 = (f32[1,16,512]{2,1,0:T(8,128)S(1)}, f32[1,16,512]{2,1,0:T(8,128)S(1)}, u32[]{:S(2)}, u32[]{:S(2)}) collective-permute-start(f32[1,16,512]{2,1,0:T(8,128)S(1)} %get-tuple-element.47), channel_id=1, source_target_pairs={{0,8},{8,16},{16,24},{24,32},{32,40},{40,48},{48,56},{56,64},{64,7... | collective-permute-start | bytes 98312 | tf_op jit(solution)/shard_map/ppermute | solution.py:29
  17.0 1.9 %collective-permute-start.5 = (f32[8,1,512]{2,1,0:T(1,128)S(1)}, f32[8,1,512]{2,1,0:T(1,128)S(1)}, u32[]{:S(2)}, u32[]{:S(2)}) collective-permute-start(f32[8,1,512]{2,1,0:T(1,128)S(1)} %get-tuple-element.44), channel_id=1, source_target_pairs={{1,0},{2,1},{3,2},{4,3},{5,4},{6,5},{7,6},{9,8},{10,9},{11,10},{12... | collective-permute-start | bytes 49160 | tf_op jit(solution)/shard_map/ppermute | solution.py:30
  18.9 4.6 %collective-permute-start.2 = (f32[8,1,512]{2,1,0:T(1,128)S(1)}, f32[8,1,512]{2,1,0:T(1,128)S(1)}, u32[]{:S(2)}, u32[]{:S(2)}) collective-permute-start(f32[8,1,512]{2,1,0:T(1,128)S(1)} %get-tuple-element.45), channel_id=1, source_target_pairs={{0,1},{1,2},{2,3},{3,4},{4,5},{5,6},{6,7},{8,9},{9,10},{10,11},{11... | collective-permute-start | bytes 49160 | tf_op jit(solution)/shard_map/ppermute | solution.py:29
  26.2 3.5 %collective-permute-start.6 = (f32[2,16,512]{2,1,0:T(8,128)S(1)}, f32[2,16,512]{2,1,0:T(8,128)S(1)}, u32[]{:S(2)}, u32[]{:S(2)}) collective-permute-start(f32[2,16,512]{2,1,0:T(8,128)S(1)} %get-tuple-element.42), channel_id=1, source_target_pairs={{0,8},{8,16},{16,24},{24,32},{32,40},{40,48},{48,56},{56,64},{64,7... | collective-permute-start | bytes 196616 | tf_op jit(solution)/shard_map/ppermute | solution.py:49
  31.1 5.0 %collective-permute-done.7 = f32[2,16,512]{2,1,0:T(8,128)S(1)} collective-permute-done((f32[2,16,512]{2,1,0:T(8,128)S(1)}, f32[2,16,512]{2,1,0:T(8,128)S(1)}, u32[]{:S(2)}, u32[]{:S(2)}) %collective-permute-start.7) | collective-permute-done | bytes 65568 | tf_op jit(solution)/shard_map/ppermute | solution.py:51
  36.1 5.4 %collective-permute-start.8 = (f32[12,2,512]{2,1,0:T(2,128)S(1)}, f32[12,2,512]{2,1,0:T(2,128)S(1)}, u32[]{:S(2)}, u32[]{:S(2)}) collective-permute-start(f32[12,2,512]{2,1,0:T(2,128)S(1)} %get-tuple-element.32), channel_id=1, source_target_pairs={{0,1},{1,2},{2,3},{3,4},{4,5},{5,6},{6,7},{8,9},{9,10},{10,11},{11... | collective-permute-start | bytes 147464 | tf_op jit(solution)/shard_map/ppermute | solution.py:49
  41.4 1.9 %collective-permute-start.9 = (f32[12,2,512]{2,1,0:T(2,128)S(1)}, f32[12,2,512]{2,1,0:T(2,128)S(1)}, u32[]{:S(2)}, u32[]{:S(2)}) collective-permute-start(f32[12,2,512]{2,1,0:T(2,128)S(1)} %get-tuple-element.33), channel_id=1, source_target_pairs={{1,0},{2,1},{3,2},{4,3},{5,4},{6,5},{7,6},{9,8},{10,9},{11,10},{12... | collective-permute-start | bytes 147464 | tf_op jit(solution)/shard_map/ppermute | solution.py:51
  43.4 3.6 %collective-permute-start.10 = (s32[8,1,512]{2,1,0:T(1,128)S(1)}, s32[8,1,512]{2,1,0:T(1,128)S(1)}, u32[]{:S(2)}, u32[]{:S(2)}) collective-permute-start(s32[8,1,512]{2,1,0:T(1,128)S(1)} %get-tuple-element.38), channel_id=1, source_target_pairs={{0,1},{1,2},{2,3},{3,4},{4,5},{5,6},{6,7},{8,9},{9,10},{10,11},{11... | collective-permute-start | bytes 49160 | tf_op jit(solution)/shard_map/ppermute | solution.py:29
  49.0 4.8 %collective-permute-start.11 = (s32[1,16,512]{2,1,0:T(8,128)S(1)}, s32[1,16,512]{2,1,0:T(8,128)S(1)}, u32[]{:S(2)}, u32[]{:S(2)}) collective-permute-start(s32[1,16,512]{2,1,0:T(8,128)S(1)} %get-tuple-element.40), channel_id=1, source_target_pairs={{0,8},{8,16},{16,24},{24,32},{32,40},{40,48},{48,56},{56,64},{64,7... | collective-permute-start | bytes 98312 | tf_op jit(solution)/shard_map/ppermute | solution.py:29
  55.3 3.5 %collective-permute-done.12 = s32[1,16,512]{2,1,0:T(8,128)S(1)} collective-permute-done((s32[1,16,512]{2,1,0:T(8,128)S(1)}, s32[1,16,512]{2,1,0:T(8,128)S(1)}, u32[]{:S(2)}, u32[]{:S(2)}) %collective-permute-start.12) | collective-permute-done | bytes 32800 | tf_op jit(solution)/shard_map/ppermute | solution.py:30
  58.8 5.5 %and_convert_fusion.2 = s32[10,18,512]{2,1,0:T(8,128)S(1)} fusion(f32[12,20,512]{2,1,0:T(8,128)S(1)} %pad_maximum_fusion, f32[2,16,512]{2,1,0:T(8,128)S(1)} %collective-permute-done.7, f32[8,16,512]{2,1,0:T(8,128)S(1)} %get-tuple-element.23, f32[2,16,512]{2,1,0:T(8,128)S(1)} %collective-permute-done.6, f32[12,2,512]{2,1,0:T(2,128)S(1)} %collective-permute-done.8, ...), kind=kLoop, calls=%fused_computation.195 | loop fusion | flops 25620480 | bytes 3284992 | tf_op jit(solution)/shard_map/convert_element_type | solution.py:97
  64.3 2.0 %convert_reduce_fusion.2 = (s32[]{:T(128)}, s32[8,16,512]{2,1,0:T(8,128)S(1)}) fusion(s32[8,16,512]{2,1,0:T(8,128)S(1)} %copy-done, s32[10,18,512]{2,1,0:T(8,128)S(1)} %and_convert_fusion.2, s32[8,16,512]{2,1,0:T(8,128)S(1)} %get-tuple-element.20), kind=kLoop, calls=%fused_computation.298 | loop fusion | flops 8781823 | bytes 2588676 | tf_op jit(solution)/shard_map/reduce_sum | solution.py:142
  66.4 3.4 %collective-permute-start.14 = (f32[2,16,512]{2,1,0:T(8,128)S(1)}, f32[2,16,512]{2,1,0:T(8,128)S(1)}, u32[]{:S(2)}, u32[]{:S(2)}) collective-permute-start(f32[2,16,512]{2,1,0:T(8,128)S(1)} %get-tuple-element.36), channel_id=1, source_target_pairs={{0,8},{8,16},{16,24},{24,32},{32,40},{40,48},{48,56},{56,64},{64,7... | collective-permute-start | bytes 196616 | tf_op jit(solution)/shard_map/ppermute | solution.py:49
  71.6 3.8 %collective-permute-done.15 = f32[2,16,512]{2,1,0:T(8,128)S(1)} collective-permute-done((f32[2,16,512]{2,1,0:T(8,128)S(1)}, f32[2,16,512]{2,1,0:T(8,128)S(1)}, u32[]{:S(2)}, u32[]{:S(2)}) %collective-permute-start.15) | collective-permute-done | bytes 65568 | tf_op jit(solution)/shard_map/ppermute | solution.py:51
  75.5 5.8 %collective-permute-start.16 = (f32[12,2,512]{2,1,0:T(2,128)S(1)}, f32[12,2,512]{2,1,0:T(2,128)S(1)}, u32[]{:S(2)}, u32[]{:S(2)}) collective-permute-start(f32[12,2,512]{2,1,0:T(2,128)S(1)} %get-tuple-element.30), channel_id=1, source_target_pairs={{0,1},{1,2},{2,3},{3,4},{4,5},{5,6},{6,7},{8,9},{9,10},{10,11},{11... | collective-permute-start | bytes 147464 | tf_op jit(solution)/shard_map/ppermute | solution.py:49
  81.3 2.1 %collective-permute-start.17 = (f32[12,2,512]{2,1,0:T(2,128)S(1)}, f32[12,2,512]{2,1,0:T(2,128)S(1)}, u32[]{:S(2)}, u32[]{:S(2)}) collective-permute-start(f32[12,2,512]{2,1,0:T(2,128)S(1)} %get-tuple-element.31), channel_id=1, source_target_pairs={{1,0},{2,1},{3,2},{4,3},{5,4},{6,5},{7,6},{9,8},{10,9},{11,10},{12... | collective-permute-start | bytes 147464 | tf_op jit(solution)/shard_map/ppermute | solution.py:51
  83.4 3.3 %collective-permute-done.17 = f32[12,2,512]{2,1,0:T(2,128)S(1)} collective-permute-done((f32[12,2,512]{2,1,0:T(2,128)S(1)}, f32[12,2,512]{2,1,0:T(2,128)S(1)}, u32[]{:S(2)}, u32[]{:S(2)}) %collective-permute-start.17) | collective-permute-done | bytes 49184 | tf_op jit(solution)/shard_map/ppermute | solution.py:51
  86.8 5.6 %and_convert_fusion.1 = s32[10,18,512]{2,1,0:T(8,128)S(1)} fusion(f32[12,20,512]{2,1,0:T(8,128)S(1)} %pad_maximum_fusion.1, f32[2,16,512]{2,1,0:T(8,128)S(1)} %collective-permute-done.15, f32[8,16,512]{2,1,0:T(8,128)S(1)} %select_select_fusion.3, f32[2,16,512]{2,1,0:T(8,128)S(1)} %collective-permute-done.14, f32[12,2,512]{2,1,0:T(2,128)S(1)} %collective-permute-done.16, ...), kind=kLoop, calls=%fused_computation.194 | loop fusion | flops 25620480 | bytes 3284992 | tf_op jit(solution)/shard_map/convert_element_type | solution.py:97
  92.4 2.1 %convert_reduce_fusion.1 = (s32[]{:T(128)}, s32[8,16,512]{2,1,0:T(8,128)S(1)}) fusion(s32[8,16,512]{2,1,0:T(8,128)S(1)} %get-tuple-element.15, s32[10,18,512]{2,1,0:T(8,128)S(1)} %and_convert_fusion.1, s32[8,16,512]{2,1,0:T(8,128)S(1)} %get-tuple-element.20), kind=kLoop, calls=%fused_computation.297 | loop fusion | flops 8781823 | bytes 2588676 | tf_op jit(solution)/shard_map/reduce_sum | solution.py:142
  94.6 2.9 %collective-permute-start.18 = (f32[2,16,512]{2,1,0:T(8,128)S(1)}, f32[2,16,512]{2,1,0:T(8,128)S(1)}, u32[]{:S(2)}, u32[]{:S(2)}) collective-permute-start(f32[2,16,512]{2,1,0:T(8,128)S(1)} %get-tuple-element.34), channel_id=1, source_target_pairs={{0,8},{8,16},{16,24},{24,32},{32,40},{40,48},{48,56},{56,64},{64,7... | collective-permute-start | bytes 196616 | tf_op jit(solution)/shard_map/ppermute | solution.py:49
  98.7 3.7 %collective-permute-done.19 = f32[2,16,512]{2,1,0:T(8,128)S(1)} collective-permute-done((f32[2,16,512]{2,1,0:T(8,128)S(1)}, f32[2,16,512]{2,1,0:T(8,128)S(1)}, u32[]{:S(2)}, u32[]{:S(2)}) %collective-permute-start.19) | collective-permute-done | bytes 65568 | tf_op jit(solution)/shard_map/ppermute | solution.py:51
  102.5 3.6 %collective-permute-start.20 = (f32[12,2,512]{2,1,0:T(2,128)S(1)}, f32[12,2,512]{2,1,0:T(2,128)S(1)}, u32[]{:S(2)}, u32[]{:S(2)}) collective-permute-start(f32[12,2,512]{2,1,0:T(2,128)S(1)} %get-tuple-element.28), channel_id=1, source_target_pairs={{0,1},{1,2},{2,3},{3,4},{4,5},{5,6},{6,7},{8,9},{9,10},{10,11},{11... | collective-permute-start | bytes 147464 | tf_op jit(solution)/shard_map/ppermute | solution.py:49
  108.0 3.5 %collective-permute-done.21 = f32[12,2,512]{2,1,0:T(2,128)S(1)} collective-permute-done((f32[12,2,512]{2,1,0:T(2,128)S(1)}, f32[12,2,512]{2,1,0:T(2,128)S(1)}, u32[]{:S(2)}, u32[]{:S(2)}) %collective-permute-start.21) | collective-permute-done | bytes 49184 | tf_op jit(solution)/shard_map/ppermute | solution.py:51
  111.6 5.6 %and_convert_fusion = s32[10,18,512]{2,1,0:T(8,128)S(1)} fusion(f32[12,20,512]{2,1,0:T(8,128)S(1)} %pad_maximum_fusion.2, f32[2,16,512]{2,1,0:T(8,128)S(1)} %collective-permute-done.19, f32[8,16,512]{2,1,0:T(8,128)S(1)} %select_select_fusion.1, f32[2,16,512]{2,1,0:T(8,128)S(1)} %collective-permute-done.18, f32[12,2,512]{2,1,0:T(2,128)S(1)} %collective-permute-done.20, ...), kind=kLoop, calls=%fused_computation.193 | loop fusion | flops 25620480 | bytes 3284992 | tf_op jit(solution)/shard_map/convert_element_type | solution.py:97
  117.1 2.7 %convert_reduce_fusion = (s32[]{:T(128)}, s32[8,16,512]{2,1,0:T(8,128)}) fusion(s32[8,16,512]{2,1,0:T(8,128)S(1)} %get-tuple-element.17, s32[10,18,512]{2,1,0:T(8,128)S(1)} %and_convert_fusion, s32[8,16,512]{2,1,0:T(8,128)S(1)} %get-tuple-element.20), kind=kLoop, calls=%fused_computation.296 | loop fusion | flops 8781823 | bytes 2588676 | tf_op jit(solution)/shard_map/reduce_sum | solution.py:142
  119.8 8.1 %all-reduce.14 = (s32[]{:T(128)}, s32[]{:T(128)}, s32[]{:T(128)}) all-reduce(s32[]{:T(128)} %get-tuple-element.18, s32[]{:T(128)} %get-tuple-element.16, s32[]{:T(128)} %get-tuple-element.14), channel_id=1, replica_groups=mesh['gz_0'=4,'gz_1'=8,'gy_0'=4,'gy_1'=2] {'gz_0'}, use_global_device_ids=true, to_apply=%region_11.12 | all-reduce | flops 3 | bytes 24 | tf_op jit(solution)/shard_map/psum | solution.py:59
  128.0 12.1 %all-reduce.12 = (s32[]{:T(128)}, s32[]{:T(128)}, s32[]{:T(128)}) all-reduce(s32[]{:T(128)} %get-tuple-element.8, s32[]{:T(128)} %get-tuple-element.9, s32[]{:T(128)} %get-tuple-element.10), channel_id=1, replica_groups=mesh['gz_0'=4,'gz_1'=8,'gy_0'=4,'gy_1'=2] {'gz_1'}, use_global_device_ids=true, to_apply=%region_12.13 | all-reduce | flops 3 | bytes 24 | tf_op jit(solution)/shard_map/psum | solution.py:59
  140.0 7.2 %all-reduce.13 = (s32[]{:T(128)}, s32[]{:T(128)}, s32[]{:T(128)}) all-reduce(s32[]{:T(128)} %get-tuple-element.2, s32[]{:T(128)} %get-tuple-element.3, s32[]{:T(128)} %get-tuple-element.4), channel_id=1, replica_groups=mesh['gz_0'=4,'gz_1'=8,'gy_0'=4,'gy_1'=2] {'gy_0'}, use_global_device_ids=true, to_apply=%region_13.14 | all-reduce | flops 3 | bytes 24 | tf_op jit(solution)/shard_map/psum | solution.py:59
  147.2 8.3 %all-reduce.15 = (s32[1]{0:T(128)}, s32[1]{0:T(128)}, s32[1]{0:T(128)}) all-reduce(s32[1]{0:T(128)} %bitcast.5, s32[1]{0:T(128)} %bitcast.4, s32[1]{0:T(128)} %bitcast.3), channel_id=1, replica_groups=mesh['gz_0'=4,'gz_1'=8,'gy_0'=4,'gy_1'=2] {'gy_1'}, use_global_device_ids=true, to_apply=%region_14.15 | all-reduce | flops 3 | bytes 24 | tf_op jit(solution)/shard_map/psum | solution.py:59
  155.5 2.5 %pad_add_fusion.2 = s32[3]{0:T(128)} fusion(s32[1]{0:T(128)} %get-tuple-element.11, s32[1]{0:T(128)} %get-tuple-element.12, s32[1]{0:T(128)} %get-tuple-element.13), kind=kLoop, calls=%fused_computation.345 | loop fusion | flops 6 | bytes 24 | tf_op jit(solution)/shard_map/stack | solution.py:144
  (55 shorter events, 16.4 us)
Async XLA Ops:
  1.9 9.3 %collective-permute-start.1 = (f32[1,16,512]{2,1,0:T(8,128)S(1)}, f32[1,16,512]{2,1,0:T(8,128)S(1)}, u32[]{:S(2)}, u32[]{:S(2)}) collective-permute-start(f32[1,16,512]{2,1,0:T(8,128)S(1)} %slice.347), channel_id=1, source_target_pairs={{0,8},{8,16},{16,24},{24,32},{32,40},{40,48},{48,56},{56,64},{64,7... | collective-permute-start | bytes 98312 | tf_op jit(solution)/shard_map/ppermute | solution.py:18
  6.3 4.9 %collective-permute-start = (f32[8,1,512]{2,1,0:T(1,128)S(1)}, f32[8,1,512]{2,1,0:T(1,128)S(1)}, u32[]{:S(2)}, u32[]{:S(2)}) collective-permute-start(f32[8,1,512]{2,1,0:T(1,128)S(1)} %slice.345), channel_id=1, source_target_pairs={{0,1},{1,2},{2,3},{3,4},{4,5},{5,6},{6,7},{8,9},{9,10},{10,11},{11... | collective-permute-start | bytes 49160 | tf_op jit(solution)/shard_map/ppermute | solution.py:18
  11.4 12.9 %collective-permute-start.4 = (f32[1,16,512]{2,1,0:T(8,128)S(1)}, f32[1,16,512]{2,1,0:T(8,128)S(1)}, u32[]{:S(2)}, u32[]{:S(2)}) collective-permute-start(f32[1,16,512]{2,1,0:T(8,128)S(1)} %get-tuple-element.46), channel_id=1, source_target_pairs={{8,0},{16,8},{24,16},{32,24},{40,32},{48,40},{56,48},{64,56},{72,6... | collective-permute-start | bytes 98312 | tf_op jit(solution)/shard_map/ppermute | solution.py:30
  12.7 11.6 %collective-permute-start.3 = (f32[1,16,512]{2,1,0:T(8,128)S(1)}, f32[1,16,512]{2,1,0:T(8,128)S(1)}, u32[]{:S(2)}, u32[]{:S(2)}) collective-permute-start(f32[1,16,512]{2,1,0:T(8,128)S(1)} %get-tuple-element.47), channel_id=1, source_target_pairs={{0,8},{8,16},{16,24},{24,32},{32,40},{40,48},{48,56},{56,64},{64,7... | collective-permute-start | bytes 98312 | tf_op jit(solution)/shard_map/ppermute | solution.py:29
  17.0 6.5 %collective-permute-start.5 = (f32[8,1,512]{2,1,0:T(1,128)S(1)}, f32[8,1,512]{2,1,0:T(1,128)S(1)}, u32[]{:S(2)}, u32[]{:S(2)}) collective-permute-start(f32[8,1,512]{2,1,0:T(1,128)S(1)} %get-tuple-element.44), channel_id=1, source_target_pairs={{1,0},{2,1},{3,2},{4,3},{5,4},{6,5},{7,6},{9,8},{10,9},{11,10},{12... | collective-permute-start | bytes 49160 | tf_op jit(solution)/shard_map/ppermute | solution.py:30
  18.9 5.4 %collective-permute-start.2 = (f32[8,1,512]{2,1,0:T(1,128)S(1)}, f32[8,1,512]{2,1,0:T(1,128)S(1)}, u32[]{:S(2)}, u32[]{:S(2)}) collective-permute-start(f32[8,1,512]{2,1,0:T(1,128)S(1)} %get-tuple-element.45), channel_id=1, source_target_pairs={{0,1},{1,2},{2,3},{3,4},{4,5},{5,6},{6,7},{8,9},{9,10},{10,11},{11... | collective-permute-start | bytes 49160 | tf_op jit(solution)/shard_map/ppermute | solution.py:29
  24.7 1.0 copy-start
  24.7 1.0 copy-start.1
  26.2 4.9 %collective-permute-start.6 = (f32[2,16,512]{2,1,0:T(8,128)S(1)}, f32[2,16,512]{2,1,0:T(8,128)S(1)}, u32[]{:S(2)}, u32[]{:S(2)}) collective-permute-start(f32[2,16,512]{2,1,0:T(8,128)S(1)} %get-tuple-element.42), channel_id=1, source_target_pairs={{0,8},{8,16},{16,24},{24,32},{32,40},{40,48},{48,56},{56,64},{64,7... | collective-permute-start | bytes 196616 | tf_op jit(solution)/shard_map/ppermute | solution.py:49
  29.7 6.3 %collective-permute-start.7 = (f32[2,16,512]{2,1,0:T(8,128)S(1)}, f32[2,16,512]{2,1,0:T(8,128)S(1)}, u32[]{:S(2)}, u32[]{:S(2)}) collective-permute-start(f32[2,16,512]{2,1,0:T(8,128)S(1)} %get-tuple-element.43), channel_id=1, source_target_pairs={{8,0},{16,8},{24,16},{32,24},{40,32},{48,40},{56,48},{64,56},{72,6... | collective-permute-start | bytes 196616 | tf_op jit(solution)/shard_map/ppermute | solution.py:51
  36.1 17.7 %collective-permute-start.8 = (f32[12,2,512]{2,1,0:T(2,128)S(1)}, f32[12,2,512]{2,1,0:T(2,128)S(1)}, u32[]{:S(2)}, u32[]{:S(2)}) collective-permute-start(f32[12,2,512]{2,1,0:T(2,128)S(1)} %get-tuple-element.32), channel_id=1, source_target_pairs={{0,1},{1,2},{2,3},{3,4},{4,5},{5,6},{6,7},{8,9},{9,10},{10,11},{11... | collective-permute-start | bytes 147464 | tf_op jit(solution)/shard_map/ppermute | solution.py:49
  41.4 13.7 %collective-permute-start.9 = (f32[12,2,512]{2,1,0:T(2,128)S(1)}, f32[12,2,512]{2,1,0:T(2,128)S(1)}, u32[]{:S(2)}, u32[]{:S(2)}) collective-permute-start(f32[12,2,512]{2,1,0:T(2,128)S(1)} %get-tuple-element.33), channel_id=1, source_target_pairs={{1,0},{2,1},{3,2},{4,3},{5,4},{6,5},{7,6},{9,8},{10,9},{11,10},{12... | collective-permute-start | bytes 147464 | tf_op jit(solution)/shard_map/ppermute | solution.py:51
  43.4 11.9 %collective-permute-start.10 = (s32[8,1,512]{2,1,0:T(1,128)S(1)}, s32[8,1,512]{2,1,0:T(1,128)S(1)}, u32[]{:S(2)}, u32[]{:S(2)}) collective-permute-start(s32[8,1,512]{2,1,0:T(1,128)S(1)} %get-tuple-element.38), channel_id=1, source_target_pairs={{0,1},{1,2},{2,3},{3,4},{4,5},{5,6},{6,7},{8,9},{9,10},{10,11},{11... | collective-permute-start | bytes 49160 | tf_op jit(solution)/shard_map/ppermute | solution.py:29
  47.0 8.2 %collective-permute-start.13 = (s32[8,1,512]{2,1,0:T(1,128)S(1)}, s32[8,1,512]{2,1,0:T(1,128)S(1)}, u32[]{:S(2)}, u32[]{:S(2)}) collective-permute-start(s32[8,1,512]{2,1,0:T(1,128)S(1)} %get-tuple-element.39), channel_id=1, source_target_pairs={{1,0},{2,1},{3,2},{4,3},{5,4},{6,5},{7,6},{9,8},{10,9},{11,10},{12... | collective-permute-start | bytes 49160 | tf_op jit(solution)/shard_map/ppermute | solution.py:30
  49.0 6.3 %collective-permute-start.11 = (s32[1,16,512]{2,1,0:T(8,128)S(1)}, s32[1,16,512]{2,1,0:T(8,128)S(1)}, u32[]{:S(2)}, u32[]{:S(2)}) collective-permute-start(s32[1,16,512]{2,1,0:T(8,128)S(1)} %get-tuple-element.40), channel_id=1, source_target_pairs={{0,8},{8,16},{16,24},{24,32},{32,40},{40,48},{48,56},{56,64},{64,7... | collective-permute-start | bytes 98312 | tf_op jit(solution)/shard_map/ppermute | solution.py:29
  53.8 4.9 %collective-permute-start.12 = (s32[1,16,512]{2,1,0:T(8,128)S(1)}, s32[1,16,512]{2,1,0:T(8,128)S(1)}, u32[]{:S(2)}, u32[]{:S(2)}) collective-permute-start(s32[1,16,512]{2,1,0:T(8,128)S(1)} %get-tuple-element.41), channel_id=1, source_target_pairs={{8,0},{16,8},{24,16},{32,24},{40,32},{48,40},{56,48},{64,56},{72,6... | collective-permute-start | bytes 98312 | tf_op jit(solution)/shard_map/ppermute | solution.py:30
  66.4 5.2 %collective-permute-start.14 = (f32[2,16,512]{2,1,0:T(8,128)S(1)}, f32[2,16,512]{2,1,0:T(8,128)S(1)}, u32[]{:S(2)}, u32[]{:S(2)}) collective-permute-start(f32[2,16,512]{2,1,0:T(8,128)S(1)} %get-tuple-element.36), channel_id=1, source_target_pairs={{0,8},{8,16},{16,24},{24,32},{32,40},{40,48},{48,56},{56,64},{64,7... | collective-permute-start | bytes 196616 | tf_op jit(solution)/shard_map/ppermute | solution.py:49
  69.8 5.7 %collective-permute-start.15 = (f32[2,16,512]{2,1,0:T(8,128)S(1)}, f32[2,16,512]{2,1,0:T(8,128)S(1)}, u32[]{:S(2)}, u32[]{:S(2)}) collective-permute-start(f32[2,16,512]{2,1,0:T(8,128)S(1)} %get-tuple-element.37), channel_id=1, source_target_pairs={{8,0},{16,8},{24,16},{32,24},{40,32},{48,40},{56,48},{64,56},{72,6... | collective-permute-start | bytes 196616 | tf_op jit(solution)/shard_map/ppermute | solution.py:51
  75.5 7.9 %collective-permute-start.16 = (f32[12,2,512]{2,1,0:T(2,128)S(1)}, f32[12,2,512]{2,1,0:T(2,128)S(1)}, u32[]{:S(2)}, u32[]{:S(2)}) collective-permute-start(f32[12,2,512]{2,1,0:T(2,128)S(1)} %get-tuple-element.30), channel_id=1, source_target_pairs={{0,1},{1,2},{2,3},{3,4},{4,5},{5,6},{6,7},{8,9},{9,10},{10,11},{11... | collective-permute-start | bytes 147464 | tf_op jit(solution)/shard_map/ppermute | solution.py:49
  81.3 5.4 %collective-permute-start.17 = (f32[12,2,512]{2,1,0:T(2,128)S(1)}, f32[12,2,512]{2,1,0:T(2,128)S(1)}, u32[]{:S(2)}, u32[]{:S(2)}) collective-permute-start(f32[12,2,512]{2,1,0:T(2,128)S(1)} %get-tuple-element.31), channel_id=1, source_target_pairs={{1,0},{2,1},{3,2},{4,3},{5,4},{6,5},{7,6},{9,8},{10,9},{11,10},{12... | collective-permute-start | bytes 147464 | tf_op jit(solution)/shard_map/ppermute | solution.py:51
  94.6 4.2 %collective-permute-start.18 = (f32[2,16,512]{2,1,0:T(8,128)S(1)}, f32[2,16,512]{2,1,0:T(8,128)S(1)}, u32[]{:S(2)}, u32[]{:S(2)}) collective-permute-start(f32[2,16,512]{2,1,0:T(8,128)S(1)} %get-tuple-element.34), channel_id=1, source_target_pairs={{0,8},{8,16},{16,24},{24,32},{32,40},{40,48},{48,56},{56,64},{64,7... | collective-permute-start | bytes 196616 | tf_op jit(solution)/shard_map/ppermute | solution.py:49
  97.4 5.0 %collective-permute-start.19 = (f32[2,16,512]{2,1,0:T(8,128)S(1)}, f32[2,16,512]{2,1,0:T(8,128)S(1)}, u32[]{:S(2)}, u32[]{:S(2)}) collective-permute-start(f32[2,16,512]{2,1,0:T(8,128)S(1)} %get-tuple-element.35), channel_id=1, source_target_pairs={{8,0},{16,8},{24,16},{32,24},{40,32},{48,40},{56,48},{64,56},{72,6... | collective-permute-start | bytes 196616 | tf_op jit(solution)/shard_map/ppermute | solution.py:51
  102.5 5.5 %collective-permute-start.20 = (f32[12,2,512]{2,1,0:T(2,128)S(1)}, f32[12,2,512]{2,1,0:T(2,128)S(1)}, u32[]{:S(2)}, u32[]{:S(2)}) collective-permute-start(f32[12,2,512]{2,1,0:T(2,128)S(1)} %get-tuple-element.28), channel_id=1, source_target_pairs={{0,1},{1,2},{2,3},{3,4},{4,5},{5,6},{6,7},{8,9},{9,10},{10,11},{11... | collective-permute-start | bytes 147464 | tf_op jit(solution)/shard_map/ppermute | solution.py:49
  106.0 5.4 %collective-permute-start.21 = (f32[12,2,512]{2,1,0:T(2,128)S(1)}, f32[12,2,512]{2,1,0:T(2,128)S(1)}, u32[]{:S(2)}, u32[]{:S(2)}) collective-permute-start(f32[12,2,512]{2,1,0:T(2,128)S(1)} %get-tuple-element.29), channel_id=1, source_target_pairs={{1,0},{2,1},{3,2},{4,3},{5,4},{6,5},{7,6},{9,8},{10,9},{11,10},{12... | collective-permute-start | bytes 147464 | tf_op jit(solution)/shard_map/ppermute | solution.py:51
where the time goes:
time: 159 us; the launch traced here: 158 us
  starting transfers between devices  66.4 us (42%)
  blocking collectives  35.6 us (22%)
  other arithmetic  29.7 us (19%)
  waiting for transfers between devices  25 us (16%)
    psum x4, blocking collectives, one_axis_at_a_time(): return functools.reduce(lax.psum, axes, x)  35.6 us
    ppermute x6, starting transfers between devices, extended(): lax.ppermute(tail, axis, [(i, (i + 1) % count) for i in range(ends)])  24.5 us
    ppermute x6, waiting for transfers between devices, extended(): lax.ppermute(head, axis, [((i + 1) % count, i) for i in range(ends)])  19.3 us
    ppermute x4, starting transfers between devices, padded(): lax.ppermute(last, axis, up)  17.2 us
    convert_element_type x3, other arithmetic, select(): return ((center >= 0) & (center > nearest)).astype(jnp.int32)  16.7 us
    ppermute x6, starting transfers between devices, extended(): lax.ppermute(head, axis, [((i + 1) % count, i) for i in range(ends)])  9.82 us
    ppermute x2, starting transfers between devices, passed_along(): lax.ppermute(value, axis, [(source, source + steps) for source in range(i...  8.41 us
    reduce_sum x3, other arithmetic, per_device(): local = jnp.sum((state == 0).astype(jnp.int32))  6.76 us
  transfers between devices with their start and end apart: 22, of which 9 were waited for; matrix products, arithmetic and copies ran while one was open for 0% of the time, Pallas kernels for 0%

commit v1 on v0

v1 whole, which is shorter than its diff:
```python
import functools

import jax
import jax.numpy as jnp
from jax import lax
from jax.experimental import pallas as pl
from jax.experimental.pallas import tpu as pltpu
from jax.sharding import PartitionSpec as P

ROUNDS = 3
MESH = pl.DeviceIdType.MESH
UP_UP, UP_DOWN, DOWN_UP, DOWN_DOWN = (1, 1), (1, -1), (-1, 1), (-1, -1)
DIAGONALS = (UP_UP, UP_DOWN, DOWN_UP, DOWN_DOWN)
DIRECTIONS = ((1, 0), (-1, 0), (0, 1), (0, -1)) + DIAGONALS
NONE = -3.0
LINK_Y, DEP_Y = 1 << 12, 1 << 13


def kernel(
    nz, ny,
    ranks_hbm, seeds_hbm, flags_hbm,
    state_ref, totals_ref,
    ranks, seeds, flags,
    bits, partial, rowmax, below, edge_y_out, edge_y_in, edge_d_out, edge_d_in,
    packed, near, near_halo, newc, row_out, row_in, diag_out, diag_in,
    column, whole,
    load_sem, edge_send, edge_recv, round_send, round_recv, col_send, col_recv, all_send, all_recv,
):
    gz, gy = lax.axis_index("gz"), lax.axis_index("gy")
    depth, rows, width = ranks.shape
    top, end = depth - 1, rows - 1

    loads = [
        pltpu.make_async_copy(seeds_hbm, seeds, load_sem.at[0]),
        pltpu.make_async_copy(ranks_hbm, ranks, load_sem.at[1]),
        pltpu.make_async_copy(flags_hbm, flags, load_sem.at[2]),
    ]
    for load in loads:
        load.start()

    def exists(dz, dy):
        here = None
        for at, step, count in ((gz, dz, nz), (gy, dy, ny)):
            if step:
                inside = at < count - 1 if step > 0 else at > 0
                here = inside if here is None else here & inside
        return here

    there = {d: exists(*d) for d in DIRECTIONS}
    target = {d: (gz + d[0], gy + d[1]) for d in DIRECTIONS}

    barrier = pltpu.get_barrier_semaphore()
    for d in DIAGONALS:
        @pl.when(there[d])
        def _(d=d):
            pl.semaphore_signal(barrier, inc=1, device_id=target[d], device_id_type=MESH)

    @pl.loop(1, nz)
    def _(k):
        pl.semaphore_signal(barrier, inc=1, device_id=(lax.rem(gz + k, nz), gy), device_id_type=MESH)

    @pl.loop(1, ny)
    def _(k):
        pl.semaphore_signal(barrier, inc=1, device_id=(gz, lax.rem(gy + k, ny)), device_id_type=MESH)

    def one(flag):
        return jnp.where(flag, 1, 0).astype(jnp.int32)

    sides_z = one(there[(1, 0)]) + one(there[(-1, 0)])
    sides_y = one(there[(0, 1)]) + one(there[(0, -1)])

    def fill(direction, *refs_values):
        @pl.when(jnp.logical_not(there[direction]))
        def _():
            for ref, value in refs_values:
                ref[...] = jnp.full(ref.shape, value, ref.dtype)

    fill((-1, 0), (below, 0.0), (partial.at[0], 0.0), *[(packed.at[r, 0], NONE) for r in range(ROUNDS)],
         *[(near_halo.at[r, 0], NONE) for r in range(ROUNDS)])
    fill((1, 0), (partial.at[depth + 1], 0.0), *[(packed.at[r, depth + 1], NONE) for r in range(ROUNDS)],
         *[(near_halo.at[r, 1], NONE) for r in range(ROUNDS)])
    fill((0, -1), (edge_y_in.at[0:2], 0.0), *[(row_in.at[r, 0], NONE) for r in range(ROUNDS)])
    fill((0, 1), (edge_y_in.at[2:3], 0.0), *[(row_in.at[r, 1], NONE) for r in range(ROUNDS)])
    fill(DOWN_DOWN, (edge_d_in.at[0:2], 0.0))
    fill(DOWN_UP, (edge_d_in.at[2:3], 0.0))
    fill(UP_DOWN, (edge_d_in.at[3:4], 0.0))
    for i, d in enumerate(DIAGONALS):
        fill((-d[0], -d[1]), *[(diag_in.at[r, i], NONE) for r in range(ROUNDS)])

    pl.semaphore_wait(barrier, nz - 1 + ny - 1 + sides_z * sides_y)

    started = []

    def remote(direction, source, target_ref, send, recv):
        copy = pltpu.make_async_remote_copy(
            src_ref=source, dst_ref=target_ref, send_sem=send, recv_sem=recv,
            device_id=target[direction], device_id_type=MESH,
        )

        @pl.when(there[direction])
        def _():
            copy.start()

        started.append((direction, copy))
        return direction, copy

    def arrived(pair):
        (dz, dy), copy = pair

        @pl.when(there[(-dz, -dy)])
        def _():
            copy.wait_recv()

    xpos = lax.broadcasted_iota(jnp.int32, (rows, width), 1)
    ypos = lax.broadcasted_iota(jnp.int32, (rows, width), 0)
    first, last = ypos == 0, ypos == end

    def over(row, where, plane):
        return jnp.where(where, jnp.broadcast_to(row, plane.shape), plane)

    def east(plane):
        return pltpu.roll(plane, width - 1, 1)

    def west(plane):
        return pltpu.roll(plane, 1, 1)

    def north(plane):
        return pltpu.roll(plane, rows - 1, 0)

    def south(plane):
        return pltpu.roll(plane, 1, 0)

    zero = jnp.zeros((rows, width), jnp.float32)

    loads[0].wait()

    def in_plane(z):
        c0 = jnp.where(xpos < width - 1, seeds[0, z], 0.0)
        c2 = jnp.where(last & (gy == ny - 1), 0.0, seeds[1, z])
        c4 = seeds[2, z]
        c4 = jnp.where((gz == nz - 1) & (z == top), zero, c4)
        return c0, c2, c4

    def part(z):
        c0, c2, c4 = in_plane(z)
        m = jnp.maximum(jnp.maximum(c0, west(c0)), jnp.maximum(c2, c4))
        m = jnp.maximum(m, jnp.where(first, 0.0, south(c2)))
        if not isinstance(z, int) or z > 0:
            m = jnp.maximum(m, seeds[2, z - 1])
        partial[z + 1] = m
        edge_y_out[0, z] = seeds[1, z, end:rows, :]
        edge_y_out[1, z] = m[end:rows]
        edge_y_out[2, z] = m[0:1]

    edges = [remote((1, 0), seeds.at[2, top], below, edge_send.at[0], edge_recv.at[0])]
    part(top)
    edges.append(remote((1, 0), partial.at[depth], partial.at[0], edge_send.at[1], edge_recv.at[1]))
    part(0)
    edges.append(remote((-1, 0), partial.at[1], partial.at[depth + 1], edge_send.at[2], edge_recv.at[2]))
    edge_d_out[0] = seeds[1, top, end:rows, :]
    edge_d_out[1] = seeds[2, top, end:rows, :]
    edge_d_out[2] = seeds[2, top, 0:1, :]
    edge_d_out[3] = seeds[1, 0, end:rows, :]
    for z in range(1, top):
        part(z)
    edges.append(remote((0, 1), edge_y_out.at[0:2], edge_y_in.at[0:2], edge_send.at[3], edge_recv.at[3]))
    edges.append(remote((0, -1), edge_y_out.at[2:3], edge_y_in.at[2:3], edge_send.at[4], edge_recv.at[4]))
    edges.append(remote(UP_UP, edge_d_out.at[0:2], edge_d_in.at[0:2], edge_send.at[5], edge_recv.at[5]))
    edges.append(remote(UP_DOWN, edge_d_out.at[2:3], edge_d_in.at[2:3], edge_send.at[6], edge_recv.at[6]))
    edges.append(remote(DOWN_UP, edge_d_out.at[3:4], edge_d_in.at[3:4], edge_send.at[7], edge_recv.at[7]))

    loads[1].wait()
    loads[2].wait()
    for pair in edges:
        arrived(pair)

    for z in range(depth):
        m = jnp.maximum(partial[z + 1], jnp.where(first, jnp.broadcast_to(edge_y_in[0, z], zero.shape), 0.0))
        if z == 0:
            m = jnp.maximum(m, below[...])
        rowmax[z + 1] = m
    m = partial[0]
    rowmax[0] = jnp.maximum(m, jnp.where(first, jnp.broadcast_to(edge_d_in[0], zero.shape), 0.0))
    m = jnp.maximum(partial[depth + 1], in_plane(top)[2])
    rowmax[depth + 1] = jnp.maximum(m, jnp.where(first, jnp.broadcast_to(edge_d_in[3], zero.shape), 0.0))

    def strengths(z):
        c0, c2, c4 = in_plane(z)
        c1 = west(c0)
        c3 = over(edge_y_in[0, z], first, south(c2))
        c5 = below[...] if z == 0 else seeds[2, z - 1]
        mine = rowmax[z + 1]
        low = edge_y_in[1, z]
        high = jnp.maximum(edge_y_in[2, z], c2[end:rows])
        if z == 0:
            low = jnp.maximum(low, edge_d_in[1])
            high = jnp.maximum(high, edge_d_in[2])
        others = [
            east(mine), west(mine), over(high, last, north(mine)), over(low, first, south(mine)),
            rowmax[z + 2], rowmax[z],
        ]
        word = jnp.zeros((rows, width), jnp.int32)
        measure = ranks[z]
        outer_link = outer_dep = None
        for d, (cost, other) in enumerate(zip((c0, c1, c2, c3, c4, c5), others)):
            twice = 2.0 * cost
            depends = (cost > 0) & (twice >= mine)
            feeds = (cost > 0) & (twice >= other)
            measure = jnp.where(feeds, 2.0 * measure, measure)
            link = depends | feeds
            if d in (2, 3):
                border = last if d == 2 else first
                outer = jnp.where(link & border, LINK_Y, 0) + jnp.where(depends & border, DEP_Y, 0)
                word = word + outer
                link = link & jnp.logical_not(border)
                depends = depends & jnp.logical_not(border)
            word = word + jnp.where(link, 1 << d, 0) + jnp.where(depends, 1 << (d + 6), 0)
        bits[z] = word
        flag = flags[z]
        packed[0, z + 1] = jnp.where(flag == 0, measure, jnp.where(flag == 2, -2.0, -1.0))

    def linked(word, mask, value):
        return jnp.where((word & mask) != 0, value, NONE)

    def near_inside(r, z):
        word, here = bits[z], packed[r, z + 1]
        m = jnp.maximum(linked(word, 1, east(here)), linked(word, 2, west(here)))
        m = jnp.maximum(m, linked(word, 4, north(here)))
        m = jnp.maximum(m, linked(word, 8, south(here)))
        if z < top:
            m = jnp.maximum(m, linked(word, 16, packed[r, z + 2]))
        if z > 0:
            m = jnp.maximum(m, linked(word, 32, packed[r, z]))
        near[r, z] = m
        for arr, plane in ((0, here), (1, m)):
            row_out[r, 0, arr, z] = plane[end:rows]
            row_out[r, 1, arr, z] = plane[0:1]

    def corner(r, i, d):
        z, row, z_mask = (top if d[0] > 0 else 0), (end if d[1] > 0 else 0), (16 if d[0] > 0 else 32)
        word, value = bits[z, row : row + 1, :], packed[r, z + 1, row : row + 1, :]
        diag_out[r, i, 0] = linked(word, LINK_Y, value)
        diag_out[r, i, 1] = linked(word, z_mask, value)

    def exchange(r):
        send, recv = round_send.at[r], round_recv.at[r]
        near_inside(r, top)
        near_inside(r, 0)
        copies = [
            remote((1, 0), packed.at[r, depth], packed.at[r, 0], send.at[0], recv.at[0]),
            remote((1, 0), near.at[r, top], near_halo.at[r, 0], send.at[1], recv.at[1]),
            remote((-1, 0), packed.at[r, 1], packed.at[r, depth + 1], send.at[2], recv.at[2]),
            remote((-1, 0), near.at[r, 0], near_halo.at[r, 1], send.at[3], recv.at[3]),
        ]
        for i, d in enumerate(DIAGONALS):
            corner(r, i, d)
            copies.append(remote(d, diag_out.at[r, i], diag_in.at[r, i], send.at[6 + i], recv.at[6 + i]))
        for z in range(1, top):
            near_inside(r, z)
        copies.append(remote((0, 1), row_out.at[r, 0], row_in.at[r, 0], send.at[4], recv.at[4]))
        copies.append(remote((0, -1), row_out.at[r, 1], row_in.at[r, 1], send.at[5], recv.at[5]))
        for pair in copies:
            arrived(pair)

    def yes(mask):
        return jnp.where(mask, -1, 0).astype(jnp.int32)

    def halo_rows(r, arr, z):
        low = jnp.broadcast_to(row_in[r, 0, arr, z], (rows, width))
        return over(row_in[r, 1, arr, z], last, low)

    def finish_near(r, z):
        word, here = bits[z], packed[r, z + 1]
        m = jnp.maximum(near[r, z], linked(word, LINK_Y, halo_rows(r, 0, z)))
        if z == top:
            m = jnp.maximum(m, linked(word, 16, packed[r, z + 2]))
        if z == 0:
            m = jnp.maximum(m, linked(word, 32, packed[r, z]))
        newc[z + 1] = yes((here >= 0) & (here > m))

    def outside_z(r, low):
        z, at, mask = (0, 0, 32) if low else (top, depth + 1, 16)
        there_packed, mine = packed[r, at], packed[r, z + 1]
        limit = jnp.maximum(near_halo[r, 0 if low else 1], linked(bits[z], mask, mine))
        i, j = (0, 1) if low else (2, 3)
        limit = jnp.where(first, jnp.maximum(limit, jnp.broadcast_to(diag_in[r, i, 0], limit.shape)), limit)
        limit = jnp.where(last, jnp.maximum(limit, jnp.broadcast_to(diag_in[r, j, 0], limit.shape)), limit)
        newc[at] = yes((there_packed >= 0) & (there_packed > limit))

    def update(r, z, count):
        word, here, chosen = bits[z], packed[r, z + 1], newc[z + 1]
        outer, limit = halo_rows(r, 0, z), halo_rows(r, 1, z)
        limit = jnp.maximum(limit, linked(word, LINK_Y, here))
        if z in (0, top):
            i, j = (0, 1) if z == 0 else (2, 3)
            corner_value = over(diag_in[r, j, 1], last, jnp.broadcast_to(diag_in[r, i, 1], (rows, width)))
            limit = jnp.maximum(limit, corner_value)
        hit = word & DEP_Y & yes((outer >= 0) & (outer > limit))
        for d, value in enumerate((east(chosen), west(chosen), north(chosen), south(chosen), newc[z + 2], newc[z])):
            hit = hit | (word & (1 << (d + 6)) & value)
        after = jnp.where(chosen != 0, -2.0, jnp.where((here >= 0) & (hit != 0), -1.0, here))
        if r + 1 < ROUNDS:
            packed[r + 1, z + 1] = after
        else:
            state_ref[z] = jnp.where(after >= 0, 0, jnp.where(after == -2.0, 2, 1)).astype(jnp.int32)
        return count + jnp.where(after >= 0, 1.0, 0.0)

    for z in range(depth):
        strengths(z)

    lane = lax.broadcasted_iota(jnp.int32, (1, 128), 1)
    counted = jnp.zeros((1, 128), jnp.float32)
    for r in range(ROUNDS):
        exchange(r)
        outside_z(r, True)
        outside_z(r, False)
        for z in range(depth):
            finish_near(r, z)
        count = zero
        for z in range(depth):
            count = update(r, z, count)
        counted = jnp.where(lane == r, jnp.sum(count), counted)

    column[gy] = counted

    def col_copy(k):
        return pltpu.make_async_remote_copy(
            src_ref=column.at[gy], dst_ref=column.at[gy], send_sem=col_send.at[k], recv_sem=col_recv.at[gy],
            device_id=(gz, lax.rem(gy + k, ny)), device_id_type=MESH)

    def all_copy(k):
        return pltpu.make_async_remote_copy(
            src_ref=whole.at[gz], dst_ref=whole.at[gz], send_sem=all_send.at[k], recv_sem=all_recv.at[gz],
            device_id=(lax.rem(gz + k, nz), gy), device_id_type=MESH)

    def landed(buffer, sem, me, count):
        @pl.loop(1, count)
        def _(k):
            who = lax.rem(me + k, count)
            pltpu.make_async_copy(buffer.at[who], buffer.at[who], sem.at[who]).wait()

    @pl.loop(1, ny)
    def _(k):
        col_copy(k).start()

    landed(column, col_recv, gy, ny)
    whole[gz] = jnp.sum(column[...], axis=0)

    @pl.loop(1, nz)
    def _(k):
        all_copy(k).start()

    landed(whole, all_recv, gz, nz)
    totals_ref[...] = jnp.sum(whole[...], axis=0).astype(jnp.int32)

    for (dz, dy), copy in started:
        @pl.when(there[(dz, dy)])
        def _(copy=copy):
            copy.wait_send()

    @pl.loop(1, ny)
    def _(k):
        col_copy(k).wait_send()

    @pl.loop(1, nz)
    def _(k):
        all_copy(k).wait_send()


def per_device(nz, ny, ranks, seeds, flags):
    depth, rows, width = ranks.shape
    f32, i32, vmem, dma = jnp.float32, jnp.int32, pltpu.VMEM, pltpu.SemaphoreType.DMA
    plane = (rows, width)
    scratch = [
        vmem(ranks.shape, f32), vmem(seeds.shape, f32), vmem(flags.shape, i32),
        vmem(ranks.shape, i32), vmem((depth + 2, *plane), f32), vmem((depth + 2, *plane), f32), vmem(plane, f32),
        vmem((3, depth, 1, width), f32), vmem((3, depth, 1, width), f32),
        vmem((4, 1, width), f32), vmem((4, 1, width), f32),
        vmem((ROUNDS, depth + 2, *plane), f32), vmem((ROUNDS, depth, *plane), f32), vmem((ROUNDS, 2, *plane), f32),
        vmem((depth + 2, *plane), i32),
        vmem((ROUNDS, 2, 2, depth, 1, width), f32), vmem((ROUNDS, 2, 2, depth, 1, width), f32),
        vmem((ROUNDS, 4, 2, 1, width), f32), vmem((ROUNDS, 4, 2, 1, width), f32),
        vmem((ny, 1, 128), f32), vmem((nz, 1, 128), f32),
        dma((3,)), dma((8,)), dma((8,)), dma((ROUNDS, 10)), dma((ROUNDS, 10)),
        dma((ny,)), dma((ny,)), dma((nz,)), dma((nz,)),
    ]
    state, totals = pl.pallas_call(
        functools.partial(kernel, nz, ny),
        out_shape=(jax.ShapeDtypeStruct(ranks.shape, i32), jax.ShapeDtypeStruct((1, 128), i32)),
        in_specs=[pl.BlockSpec(memory_space=pl.ANY)] * 3,
        out_specs=(pl.BlockSpec(memory_space=pltpu.VMEM), pl.BlockSpec(memory_space=pltpu.VMEM)),
        scratch_shapes=scratch,
        compiler_params=pltpu.CompilerParams(collective_id=0, has_side_effects=True),
    )(ranks, seeds, flags)
    return state, totals[0, :ROUNDS]


def solution(mesh):
    nz, ny = mesh.shape["gz"], mesh.shape["gy"]
    return jax.shard_map(
        functools.partial(per_device, nz, ny), mesh=mesh,
        in_specs=(P("gz", "gy", None), P(None, "gz", "gy", None), P("gz", "gy", None)),
        out_specs=(P("gz", "gy", None), P()), check_vma=False,
    )
```

time: 159 us -> 46.2 us (0.29)
  starting transfers between devices: 66.4 us -> 0 us
  Pallas kernels: 0 us -> 42.7 us
  blocking collectives: 35.6 us -> 0 us
  other arithmetic: 29.7 us -> 0 us
  waiting for transfers between devices: 25 us -> 0 us
  local copies, waits for them, and re-layouts: 0.18 us -> 2.75 us
    ppermute x22 -> x0, starting transfers between devices: 66.4 us -> none  [the longest x6 24.5 us: extended(): lax.ppermute(tail, axis, [(i, (i + 1) % count) for i in range(ends)])]
    pallas_call x0 -> x1, Pallas kernels: none -> 42.7 us  [per_device(): pl.pallas_call(functools.partial(kernel, nz, ny), out_shape=(jax.ShapeDty...]
    psum x4 -> x0, blocking collectives: 35.6 us -> none  [one_axis_at_a_time(): return functools.reduce(lax.psum, axes, x)]
    ppermute x22 -> x0, waiting for transfers between devices: 25 us -> none  [the longest x6 19.3 us: extended(): lax.ppermute(head, axis, [((i + 1) % count, i) for i in range(ends)])]
    convert_element_type x3 -> x0, other arithmetic: 16.7 us -> none  [select(): return ((center >= 0) & (center > nearest)).astype(jnp.int32)]
    reduce_sum x3 -> x0, other arithmetic: 6.76 us -> none  [per_device(): local = jnp.sum((state == 0).astype(jnp.int32))]
    another operation x1 -> x0, other arithmetic: 2.52 us -> none  [per_device(): undecided = jnp.stack(totals)]
    unnamed x4 -> x3, local copies, waits for them, and re-layouts: 0.01 us -> 2.24 us
  transfers between devices with their start and end apart: 22 -> 0, of which waited for: 9 -> 0; matrix products, arithmetic and copies ran while one was open for 0% -> 0% of each run, Pallas kernels for 0% -> 0%
where the time goes in v1:
time: 46.2 us; the launch traced here: 46.1 us
  Pallas kernels  42.7 us (92%)
  local copies, waits for them, and re-layouts  2.75 us (6%)
  between operations  0.65 us (1%)
    pallas_call x1, Pallas kernels, per_device(): pl.pallas_call(functools.partial(kernel, nz, ny), out_shape=(jax.ShapeDty...  42.7 us
    unnamed x3, local copies, waits for them, and re-layouts  2.24 us

profile of v1, /device:TPU:1, one launch (start us, length us, event | category | flops | bytes accessed | tf_op | source)
XLA Modules:
  0.0 46.1 jit_solution(7503675534735568850)
XLA Ops:
  0.6 42.7 %shard_map.50 = (s32[8,16,512]{2,1,0:T(8,128)}, s32[1,128]{1,0:T(1,128)}) custom-call(f32[8,16,512]{2,1,0:T(8,128)} %ranks_hbm.1, f32[3,8,16,512]{3,2,1,0:T(8,128)} %seeds_hbm.1, s32[8,16,512]{2,1,0:T(8,128)} %flags_hbm.1), custom_call_target="tpu_custom_call" | custom-call | tf_op jit(solution)/shard_map/pallas_call | solution.py:387
  43.3 0.0 copy-start
  43.3 0.6 %copy-done = s32[1,128]{1,0:T(1,128)S(1)} copy-done((s32[1,128]{1,0:T(1,128)S(1)}, s32[1,128]{1,0:T(1,128)}, u32[]{:S(2)}) %copy-start) | copy-done | bytes 536
  43.9 0.5 %slice_bitcast_fusion = s32[3]{0:T(128)} fusion(s32[1,128]{1,0:T(1,128)S(1)} %copy-done), kind=kLoop, calls=%fused_computation | loop fusion | bytes 24 | tf_op jit(solution)/shard_map/squeeze | solution.py:395
  44.4 1.7 %copy.6 = s32[8,16,512]{2,1,0:T(8,128)} copy(s32[8,16,512]{2,1,0:T(8,128)} %get-tuple-element.8) | data formatting | bytes 524288
Async XLA Ops:
  43.3 0.6 %copy-start = (s32[1,128]{1,0:T(1,128)S(1)}, s32[1,128]{1,0:T(1,128)}, u32[]{:S(2)}) copy-start(s32[1,128]{1,0:T(1,128)} %get-tuple-element.5) | copy-start | bytes 1540

commit v2 on v1

--- a/solution.py
+++ b/solution.py
@@ -24,7 +24,7 @@
     bits, partial, rowmax, below, edge_y_out, edge_y_in, edge_d_out, edge_d_in,
     packed, near, near_halo, newc, row_out, row_in, diag_out, diag_in,
     column, whole,
-    load_sem, edge_send, edge_recv, round_send, round_recv, col_send, col_recv, all_send, all_recv,
+    known, load_sem, edge_send, edge_recv, round_send, round_recv, col_send, col_recv, all_send, all_recv,
 ):
     gz, gy = lax.axis_index("gz"), lax.axis_index("gy")
     depth, rows, width = ranks.shape
@@ -55,19 +55,125 @@
         def _(d=d):
             pl.semaphore_signal(barrier, inc=1, device_id=target[d], device_id_type=MESH)
 
-    @pl.loop(1, nz)
-    def _(k):
-        pl.semaphore_signal(barrier, inc=1, device_id=(lax.rem(gz + k, nz), gy), device_id_type=MESH)
+    for step in (1, nz - 1):
+        pl.semaphore_signal(barrier, inc=1, device_id=(lax.rem(gz + step, nz), gy), device_id_type=MESH)
 
     @pl.loop(1, ny)
     def _(k):
         pl.semaphore_signal(barrier, inc=1, device_id=(gz, lax.rem(gy + k, ny)), device_id_type=MESH)
 
+    strides, reach = [], 1
+    while 2 * reach + 1 < nz:
+        strides.append(reach)
+        reach *= 2
+
+    def tell(i):
+        if i < len(strides):
+            for step in (strides[i], nz - strides[i]):
+                pl.semaphore_signal(known.at[i], inc=1, device_id=(lax.rem(gz + step, nz), gy), device_id_type=MESH)
+
+    def told(i):
+        if i < len(strides):
+            pl.semaphore_wait(known.at[i], 2)
+
     def one(flag):
         return jnp.where(flag, 1, 0).astype(jnp.int32)
 
     sides_z = one(there[(1, 0)]) + one(there[(-1, 0)])
     sides_y = one(there[(0, 1)]) + one(there[(0, -1)])
+
+    started = []
+
+    def remote(direction, source, target_ref, send, recv):
+        copy = pltpu.make_async_remote_copy(
+            src_ref=source, dst_ref=target_ref, send_sem=send, recv_sem=recv,
+            device_id=target[direction], device_id_type=MESH,
+        )
+
+        @pl.when(there[direction])
+        def _():
+            copy.start()
+
+        started.append((direction, copy))
+        return direction, copy
+
+    def arrived(pair):
+        (dz, dy), copy = pair
+
+        @pl.when(there[(-dz, -dy)])
+        def _():
+            copy.wait_recv()
+
+    xpos = lax.broadcasted_iota(jnp.int32, (rows, width), 1)
+    ypos = lax.broadcasted_iota(jnp.int32, (rows, width), 0)
+    first, last = ypos == 0, ypos == end
+
+    def over(row, where, plane):
+        return jnp.where(where, jnp.broadcast_to(row, plane.shape), plane)
+
+    def east(plane):
+        return pltpu.roll(plane, width - 1, 1)
+
+    def west(plane):
+        return pltpu.roll(plane, 1, 1)
+
+    def north(plane):
+        return pltpu.roll(plane, rows - 1, 0)
+
+    def south(plane):
+        return pltpu.roll(plane, 1, 0)
+
+    zero = jnp.zeros((rows, width), jnp.float32)
+
+    loads[0].wait()
+
+    def in_plane(z):
+        c0 = jnp.where(xpos < width - 1, seeds[0, z], 0.0)
+        c2 = jnp.where(last & (gy == ny - 1), 0.0, seeds[1, z])
+        c4 = seeds[2, z]
+        c4 = jnp.where((gz == nz - 1) & (z == top), zero, c4)
+        return c0, c2, c4
+
+    def part(z):
+        c0, c2, c4 = in_plane(z)
+        m = jnp.maximum(jnp.maximum(c0, west(c0)), jnp.maximum(c2, c4))
+        m = jnp.maximum(m, jnp.where(first, 0.0, south(c2)))
+        if not isinstance(z, int) or z > 0:
+            m = jnp.maximum(m, seeds[2, z - 1])
+        partial[z + 1] = m
+        edge_y_out[0, z] = seeds[1, z, end:rows, :]
+        edge_y_out[1, z] = m[end:rows]
+        edge_y_out[2, z] = m[0:1]
+
+    part(top)
+    part(0)
+    edge_d_out[0] = seeds[1, top, end:rows, :]
+    edge_d_out[1] = seeds[2, top, end:rows, :]
+    edge_d_out[2] = seeds[2, top, 0:1, :]
+    edge_d_out[3] = seeds[1, 0, end:rows, :]
+
+    pl.semaphore_wait(barrier, 2 + ny - 1 + sides_z * sides_y)
+
+    def edge(direction, source, target_ref, i):
+        return remote(direction, source, target_ref, edge_send.at[i], edge_recv.at[i])
+
+    edge_d = [
+        edge(UP_UP, edge_d_out.at[0:2], edge_d_in.at[0:2], 0),
+        edge(UP_DOWN, edge_d_out.at[2:3], edge_d_in.at[2:3], 1),
+        edge(DOWN_UP, edge_d_out.at[3:4], edge_d_in.at[3:4], 2),
+    ]
+    edge_z = [
+        edge((1, 0), seeds.at[2, top], below, 3),
+        edge((1, 0), partial.at[depth], partial.at[0], 4),
+        edge((-1, 0), partial.at[1], partial.at[depth + 1], 5),
+    ]
+    tell(0)
+    for z in range(1, top):
+        part(z)
+    edge_y = [
+        edge((0, 1), edge_y_out.at[0:2], edge_y_in.at[0:2], 6),
+        edge((0, -1), edge_y_out.at[2:3], edge_y_in.at[2:3], 7),
+    ]
 
     def fill(direction, *refs_values):
         @pl.when(jnp.logical_not(there[direction]))
@@ -87,102 +193,17 @@
     for i, d in enumerate(DIAGONALS):
         fill((-d[0], -d[1]), *[(diag_in.at[r, i], NONE) for r in range(ROUNDS)])
 
-    pl.semaphore_wait(barrier, nz - 1 + ny - 1 + sides_z * sides_y)
-
-    started = []
-
-    def remote(direction, source, target_ref, send, recv):
-        copy = pltpu.make_async_remote_copy(
-            src_ref=source, dst_ref=target_ref, send_sem=send, recv_sem=recv,
-            device_id=target[direction], device_id_type=MESH,
-        )
-
-        @pl.when(there[direction])
-        def _():
-            copy.start()
-
-        started.append((direction, copy))
-        return direction, copy
-
-    def arrived(pair):
-        (dz, dy), copy = pair
-
-        @pl.when(there[(-dz, -dy)])
-        def _():
-            copy.wait_recv()
-
-    xpos = lax.broadcasted_iota(jnp.int32, (rows, width), 1)
-    ypos = lax.broadcasted_iota(jnp.int32, (rows, width), 0)
-    first, last = ypos == 0, ypos == end
-
-    def over(row, where, plane):
-        return jnp.where(where, jnp.broadcast_to(row, plane.shape), plane)
-
-    def east(plane):
-        return pltpu.roll(plane, width - 1, 1)
-
-    def west(plane):
-        return pltpu.roll(plane, 1, 1)
-
-    def north(plane):
-        return pltpu.roll(plane, rows - 1, 0)
-
-    def south(plane):
-        return pltpu.roll(plane, 1, 0)
-
-    zero = jnp.zeros((rows, width), jnp.float32)
-
-    loads[0].wait()
-
-    def in_plane(z):
-        c0 = jnp.where(xpos < width - 1, seeds[0, z], 0.0)
-        c2 = jnp.where(last & (gy == ny - 1), 0.0, seeds[1, z])
-        c4 = seeds[2, z]
-        c4 = jnp.where((gz == nz - 1) & (z == top), zero, c4)
-        return c0, c2, c4
-
-    def part(z):
-        c0, c2, c4 = in_plane(z)
-        m = jnp.maximum(jnp.maximum(c0, west(c0)), jnp.maximum(c2, c4))
-        m = jnp.maximum(m, jnp.where(first, 0.0, south(c2)))
-        if not isinstance(z, int) or z > 0:
-            m = jnp.maximum(m, seeds[2, z - 1])
-        partial[z + 1] = m
-        edge_y_out[0, z] = seeds[1, z, end:rows, :]
-        edge_y_out[1, z] = m[end:rows]
-        edge_y_out[2, z] = m[0:1]
-
-    edges = [remote((1, 0), seeds.at[2, top], below, edge_send.at[0], edge_recv.at[0])]
-    part(top)
-    edges.append(remote((1, 0), partial.at[depth], partial.at[0], edge_send.at[1], edge_recv.at[1]))
-    part(0)
-    edges.append(remote((-1, 0), partial.at[1], partial.at[depth + 1], edge_send.at[2], edge_recv.at[2]))
-    edge_d_out[0] = seeds[1, top, end:rows, :]
-    edge_d_out[1] = seeds[2, top, end:rows, :]
-    edge_d_out[2] = seeds[2, top, 0:1, :]
-    edge_d_out[3] = seeds[1, 0, end:rows, :]
-    for z in range(1, top):
-        part(z)
-    edges.append(remote((0, 1), edge_y_out.at[0:2], edge_y_in.at[0:2], edge_send.at[3], edge_recv.at[3]))
-    edges.append(remote((0, -1), edge_y_out.at[2:3], edge_y_in.at[2:3], edge_send.at[4], edge_recv.at[4]))
-    edges.append(remote(UP_UP, edge_d_out.at[0:2], edge_d_in.at[0:2], edge_send.at[5], edge_recv.at[5]))
-    edges.append(remote(UP_DOWN, edge_d_out.at[2:3], edge_d_in.at[2:3], edge_send.at[6], edge_recv.at[6]))
-    edges.append(remote(DOWN_UP, edge_d_out.at[3:4], edge_d_in.at[3:4], edge_send.at[7], edge_recv.at[7]))
-
-    loads[1].wait()
-    loads[2].wait()
-    for pair in edges:
-        arrived(pair)
-
-    for z in range(depth):
+    def whole_rowmax(z):
         m = jnp.maximum(partial[z + 1], jnp.where(first, jnp.broadcast_to(edge_y_in[0, z], zero.shape), 0.0))
         if z == 0:
             m = jnp.maximum(m, below[...])
         rowmax[z + 1] = m
-    m = partial[0]
-    rowmax[0] = jnp.maximum(m, jnp.where(first, jnp.broadcast_to(edge_d_in[0], zero.shape), 0.0))
-    m = jnp.maximum(partial[depth + 1], in_plane(top)[2])
-    rowmax[depth + 1] = jnp.maximum(m, jnp.where(first, jnp.broadcast_to(edge_d_in[3], zero.shape), 0.0))
+
+    def outside_rowmax():
+        m = partial[0]
+        rowmax[0] = jnp.maximum(m, jnp.where(first, jnp.broadcast_to(edge_d_in[0], zero.shape), 0.0))
+        m = jnp.maximum(partial[depth + 1], in_plane(top)[2])
+        rowmax[depth + 1] = jnp.maximum(m, jnp.where(first, jnp.broadcast_to(edge_d_in[3], zero.shape), 0.0))
 
     def strengths(z):
         c0, c2, c4 = in_plane(z)
@@ -242,25 +263,29 @@
         diag_out[r, i, 0] = linked(word, LINK_Y, value)
         diag_out[r, i, 1] = linked(word, z_mask, value)
 
-    def exchange(r):
+    def send_packed(r):
         send, recv = round_send.at[r], round_recv.at[r]
-        near_inside(r, top)
-        near_inside(r, 0)
-        copies = [
+        for i, d in enumerate(DIAGONALS):
+            corner(r, i, d)
+        return [
+            *[remote(d, diag_out.at[r, i], diag_in.at[r, i], send.at[6 + i], recv.at[6 + i]) for i, d in enumerate(DIAGONALS)],
             remote((1, 0), packed.at[r, depth], packed.at[r, 0], send.at[0], recv.at[0]),
+            remote((-1, 0), packed.at[r, 1], packed.at[r, depth + 1], send.at[2], recv.at[2]),
+        ]
+
+    def send_near(r):
+        send, recv = round_send.at[r], round_recv.at[r]
+        return [
             remote((1, 0), near.at[r, top], near_halo.at[r, 0], send.at[1], recv.at[1]),
-            remote((-1, 0), packed.at[r, 1], packed.at[r, depth + 1], send.at[2], recv.at[2]),
             remote((-1, 0), near.at[r, 0], near_halo.at[r, 1], send.at[3], recv.at[3]),
         ]
-        for i, d in enumerate(DIAGONALS):
-            corner(r, i, d)
-            copies.append(remote(d, diag_out.at[r, i], diag_in.at[r, i], send.at[6 + i], recv.at[6 + i]))
-        for z in range(1, top):
-            near_inside(r, z)
-        copies.append(remote((0, 1), row_out.at[r, 0], row_in.at[r, 0], send.at[4], recv.at[4]))
-        copies.append(remote((0, -1), row_out.at[r, 1], row_in.at[r, 1], send.at[5], recv.at[5]))
-        for pair in copies:
-            arrived(pair)
+
+    def send_rows(r):
+        send, recv = round_send.at[r], round_recv.at[r]
+        return [
+            remote((0, 1), row_out.at[r, 0], row_in.at[r, 0], send.at[4], recv.at[4]),
+            remote((0, -1), row_out.at[r, 1], row_in.at[r, 1], send.at[5], recv.at[5]),
+        ]
 
     def yes(mask):
         return jnp.where(mask, -1, 0).astype(jnp.int32)
@@ -305,20 +330,60 @@
             state_ref[z] = jnp.where(after >= 0, 0, jnp.where(after == -2.0, 2, 1)).astype(jnp.int32)
         return count + jnp.where(after >= 0, 1.0, 0.0)
 
-    for z in range(depth):
+    def wait_all(pairs):
+        for pair in pairs:
+            arrived(pair)
+
+    inner, middle = range(1, top), range(2, top - 1)
+    loads[1].wait()
+    loads[2].wait()
+    wait_all(edge_y)
+    for z in inner:
+        whole_rowmax(z)
+    for z in middle:
         strengths(z)
+    wait_all(edge_z)
+    wait_all(edge_d)
+    whole_rowmax(0)
+    whole_rowmax(top)
+    outside_rowmax()
+    strengths(0)
+    strengths(top)
+    told(0)
+    tell(1)
 
     lane = lax.broadcasted_iota(jnp.int32, (1, 128), 1)
     counted = jnp.zeros((1, 128), jnp.float32)
     for r in range(ROUNDS):
-        exchange(r)
+        sent_packed = send_packed(r)
+        if r == 0:
+            strengths(1)
+            strengths(top - 1)
+        near_inside(r, 0)
+        near_inside(r, top)
+        sent_near = send_near(r)
+        for z in inner:
+            near_inside(r, z)
+        sent_rows = send_rows(r)
+
+        wait_all(sent_rows)
+        for z in inner:
+            finish_near(r, z)
+        count = zero
+        for z in middle:
+            count = update(r, z, count)
+        wait_all(sent_packed)
+        finish_near(r, 0)
+        finish_near(r, top)
+        count = update(r, 1, count)
+        count = update(r, top - 1, count)
+        wait_all(sent_near)
         outside_z(r, True)
         outside_z(r, False)
-        for z in range(depth):
-            finish_near(r, z)
-        count = zero
-        for z in range(depth):
-            count = update(r, z, count)
+        count = update(r, 0, count)
+        count = update(r, top, count)
+        told(r + 1)
+        tell(r + 2)
         counted = jnp.where(lane == r, jnp.sum(count), counted)
 
     column[gy] = counted
@@ -351,7 +416,7 @@
         all_copy(k).start()
 
     landed(whole, all_recv, gz, nz)
-    totals_ref[...] = jnp.sum(whole[...], axis=0).astype(jnp.int32)
+    totals_ref[...] = jnp.sum(whole[...], axis=0)
 
     for (dz, dy), copy in started:
         @pl.when(there[(dz, dy)])
@@ -365,6 +430,16 @@
     @pl.loop(1, nz)
     def _(k):
         all_copy(k).wait_send()
+
+
+def deliver(state, totals, state_out, totals_out, sem):
+    copy = pltpu.make_async_copy(state, state_out, sem)
+    copy.start()
+    row = totals[...]
+    lane = lax.broadcasted_iota(jnp.int32, row.shape, 1)
+    for r in range(ROUNDS):
+        totals_out[r] = jnp.sum(jnp.where(lane == r, row, 0.0)).astype(jnp.int32)
+    copy.wait()
 
 
 def per_device(nz, ny, ranks, seeds, flags):
@@ -381,18 +456,24 @@
         vmem((ROUNDS, 2, 2, depth, 1, width), f32), vmem((ROUNDS, 2, 2, depth, 1, width), f32),
         vmem((ROUNDS, 4, 2, 1, width), f32), vmem((ROUNDS, 4, 2, 1, width), f32),
         vmem((ny, 1, 128), f32), vmem((nz, 1, 128), f32),
-        dma((3,)), dma((8,)), dma((8,)), dma((ROUNDS, 10)), dma((ROUNDS, 10)),
+        pltpu.SemaphoreType.REGULAR((4,)), dma((3,)), dma((8,)), dma((8,)), dma((ROUNDS, 10)), dma((ROUNDS, 10)),
         dma((ny,)), dma((ny,)), dma((nz,)), dma((nz,)),
     ]
     state, totals = pl.pallas_call(
         functools.partial(kernel, nz, ny),
-        out_shape=(jax.ShapeDtypeStruct(ranks.shape, i32), jax.ShapeDtypeStruct((1, 128), i32)),
+        out_shape=(vmem(ranks.shape, i32), vmem((1, 128), f32)),
         in_specs=[pl.BlockSpec(memory_space=pl.ANY)] * 3,
         out_specs=(pl.BlockSpec(memory_space=pltpu.VMEM), pl.BlockSpec(memory_space=pltpu.VMEM)),
         scratch_shapes=scratch,
         compiler_params=pltpu.CompilerParams(collective_id=0, has_side_effects=True),
     )(ranks, seeds, flags)
-    return state, totals[0, :ROUNDS]
+    return pl.pallas_call(
+        deliver,
+        out_shape=(jax.ShapeDtypeStruct(ranks.shape, i32), jax.ShapeDtypeStruct((ROUNDS,), i32)),
+        in_specs=[pl.BlockSpec(memory_space=pltpu.VMEM)] * 2,
+        out_specs=(pl.BlockSpec(memory_space=pl.ANY), pl.BlockSpec(memory_space=pltpu.SMEM)),
+        scratch_shapes=[dma],
+    )(*[pltpu.with_memory_space_constraint(x, pltpu.VMEM) for x in (state, totals)])
 
 
 def solution(mesh):

time: 46.2 us -> 39.1 us (0.85)
  Pallas kernels: 42.7 us -> 38.3 us
  local copies, waits for them, and re-layouts: 2.75 us -> 0 us
    pallas_call x1 -> x2, Pallas kernels: 42.7 us -> 38.3 us  [the longest x1 37.1 us: per_device(): pl.pallas_call(functools.partial(kernel, nz, ny), out_shape=(vmem(ranks.s...]
    unnamed x3 -> x0, local copies, waits for them, and re-layouts: 2.24 us -> none
    squeeze x1 -> x0, local copies, waits for them, and re-layouts: 0.51 us -> none  [per_device(): return (state, totals[0, :ROUNDS])]
where the time goes in v2:
time: 39.1 us; the launch traced here: 39 us
  Pallas kernels  38.3 us (98%)
  between operations  0.64 us (2%)
    pallas_call x1, Pallas kernels, per_device(): pl.pallas_call(functools.partial(kernel, nz, ny), out_shape=(vmem(ranks.s...  37.1 us
    pallas_call x1, Pallas kernels, per_device(): pl.pallas_call(deliver, out_shape=(jax.ShapeDtypeStruct(ranks.shape, i32)...  1.23 us

profile of v2, /device:TPU:1, one launch (start us, length us, event | category | flops | bytes accessed | tf_op | source)
XLA Modules:
  0.0 39.0 jit_solution(2018507409105083305)
XLA Ops:
  0.6 37.1 %shard_map.50 = (s32[8,16,512]{2,1,0:T(8,128)S(1)}, f32[1,128]{1,0:T(1,128)S(1)}) custom-call(f32[8,16,512]{2,1,0:T(8,128)} %ranks_hbm.1, f32[3,8,16,512]{3,2,1,0:T(8,128)} %seeds_hbm.1, s32[8,16,512]{2,1,0:T(8,128)} %flags_hbm.1), custom_call_target="tpu_custom_call" | custom-call | tf_op jit(solution)/shard_map/pallas_call | solution.py:462
  37.7 1.2 %shard_map.51 = (s32[8,16,512]{2,1,0:T(8,128)}, s32[3]{0:T(128)}) custom-call(s32[8,16,512]{2,1,0:T(8,128)S(1)} %get-tuple-element.4.state, f32[1,128]{1,0:T(1,128)S(1)} %get-tuple-element.5.totals), custom_call_target="tpu_custom_call" | custom-call | tf_op jit(solution)/shard_map/pallas_call | solution.py:470

commit v3 on v2

--- a/solution.py
+++ b/solution.py
@@ -23,8 +23,8 @@
     ranks, seeds, flags,
     bits, partial, rowmax, below, edge_y_out, edge_y_in, edge_d_out, edge_d_in,
     packed, near, near_halo, newc, row_out, row_in, diag_out, diag_in,
-    column, whole,
-    known, load_sem, edge_send, edge_recv, round_send, round_recv, col_send, col_recv, all_send, all_recv,
+    couple, whole,
+    known, load_sem, edge_send, edge_recv, round_send, round_recv, pair_send, pair_recv, all_send, all_recv,
 ):
     gz, gy = lax.axis_index("gz"), lax.axis_index("gy")
     depth, rows, width = ranks.shape
@@ -63,7 +63,7 @@
         pl.semaphore_signal(barrier, inc=1, device_id=(gz, lax.rem(gy + k, ny)), device_id_type=MESH)
 
     strides, reach = [], 1
-    while 2 * reach + 1 < nz:
+    while 2 * reach - 1 < nz:
         strides.append(reach)
         reach *= 2
 
@@ -367,6 +367,9 @@
         sent_rows = send_rows(r)
 
         wait_all(sent_rows)
+        if r == ROUNDS - 1:
+            told(r + 1)
+            tell(r + 2)
         for z in inner:
             finish_near(r, z)
         count = zero
@@ -382,54 +385,47 @@
         outside_z(r, False)
         count = update(r, 0, count)
         count = update(r, top, count)
-        told(r + 1)
-        tell(r + 2)
+        if r < ROUNDS - 1:
+            told(r + 1)
+            tell(r + 2)
         counted = jnp.where(lane == r, jnp.sum(count), counted)
 
-    column[gy] = counted
-
-    def col_copy(k):
+    half = ny // 2
+    lone, core = gz * half + gy // 2, lax.rem(gy, 2)
+    couple[core] = counted
+    to_partner = pltpu.make_async_remote_copy(
+        src_ref=couple.at[core], dst_ref=couple.at[core], send_sem=pair_send, recv_sem=pair_recv,
+        device_id=(gz, gy + 1 - 2 * core), device_id_type=MESH)
+    to_partner.start()
+    to_partner.wait_recv()
+    told(ROUNDS + 1)
+    whole[lone] = couple[0] + couple[1]
+
+    def all_copy(kz, ky):
         return pltpu.make_async_remote_copy(
-            src_ref=column.at[gy], dst_ref=column.at[gy], send_sem=col_send.at[k], recv_sem=col_recv.at[gy],
-            device_id=(gz, lax.rem(gy + k, ny)), device_id_type=MESH)
-
-    def all_copy(k):
-        return pltpu.make_async_remote_copy(
-            src_ref=whole.at[gz], dst_ref=whole.at[gz], send_sem=all_send.at[k], recv_sem=all_recv.at[gz],
-            device_id=(lax.rem(gz + k, nz), gy), device_id_type=MESH)
-
-    def landed(buffer, sem, me, count):
-        @pl.loop(1, count)
-        def _(k):
-            who = lax.rem(me + k, count)
-            pltpu.make_async_copy(buffer.at[who], buffer.at[who], sem.at[who]).wait()
-
-    @pl.loop(1, ny)
-    def _(k):
-        col_copy(k).start()
-
-    landed(column, col_recv, gy, ny)
-    whole[gz] = jnp.sum(column[...], axis=0)
-
-    @pl.loop(1, nz)
-    def _(k):
-        all_copy(k).start()
-
-    landed(whole, all_recv, gz, nz)
+            src_ref=whole.at[lone], dst_ref=whole.at[lone], send_sem=all_send, recv_sem=all_recv,
+            device_id=(lax.rem(gz + kz, nz), lax.rem(gy + 2 * ky, ny)), device_id_type=MESH)
+
+    @pl.loop(0, nz)
+    def _(i):
+        kz = lax.rem(i + 4, nz)
+        for ky in range(1, half):
+            all_copy(kz, ky).start()
+
+        @pl.when(kz > 0)
+        def _():
+            all_copy(kz, 0).start()
+
+    others = whole.at[0 : nz * half - 1]
+    pltpu.make_async_copy(others, others, all_recv).wait()
     totals_ref[...] = jnp.sum(whole[...], axis=0)
+    pltpu.make_async_copy(others, others, all_send).wait()
+    to_partner.wait_send()
 
     for (dz, dy), copy in started:
         @pl.when(there[(dz, dy)])
         def _(copy=copy):
             copy.wait_send()
-
-    @pl.loop(1, ny)
-    def _(k):
-        col_copy(k).wait_send()
-
-    @pl.loop(1, nz)
-    def _(k):
-        all_copy(k).wait_send()
 
 
 def deliver(state, totals, state_out, totals_out, sem):
@@ -455,9 +451,9 @@
         vmem((depth + 2, *plane), i32),
         vmem((ROUNDS, 2, 2, depth, 1, width), f32), vmem((ROUNDS, 2, 2, depth, 1, width), f32),
         vmem((ROUNDS, 4, 2, 1, width), f32), vmem((ROUNDS, 4, 2, 1, width), f32),
-        vmem((ny, 1, 128), f32), vmem((nz, 1, 128), f32),
-        pltpu.SemaphoreType.REGULAR((4,)), dma((3,)), dma((8,)), dma((8,)), dma((ROUNDS, 10)), dma((ROUNDS, 10)),
-        dma((ny,)), dma((ny,)), dma((nz,)), dma((nz,)),
+        vmem((2, 1, 128), f32), vmem((nz * ny // 2, 1, 128), f32),
+        pltpu.SemaphoreType.REGULAR((ROUNDS + 2,)), dma((3,)), dma((8,)), dma((8,)), dma((ROUNDS, 10)), dma((ROUNDS, 10)),
+        dma, dma, dma, dma,
     ]
     state, totals = pl.pallas_call(
         functools.partial(kernel, nz, ny),

time: 39.1 us -> 37.5 us (0.959)
  Pallas kernels: 38.3 us -> 36.7 us
    pallas_call x1, Pallas kernels: 37.1 us -> 35.5 us  [per_device(): pl.pallas_call(functools.partial(kernel, nz, ny), out_shape=(vmem(ranks.s...]
where the time goes in v3:
time: 37.5 us; the launch traced here: 37.4 us
  Pallas kernels  36.7 us (98%)
  between operations  0.64 us (2%)
    pallas_call x1, Pallas kernels, per_device(): pl.pallas_call(functools.partial(kernel, nz, ny), out_shape=(vmem(ranks.s...  35.5 us
    pallas_call x1, Pallas kernels, per_device(): pl.pallas_call(deliver, out_shape=(jax.ShapeDtypeStruct(ranks.shape, i32)...  1.23 us

profile of v3, /device:TPU:1, one launch (start us, length us, event | category | flops | bytes accessed | tf_op | source)
XLA Modules:
  0.0 37.4 jit_solution(7419282897295895720)
XLA Ops:
  0.6 35.5 %shard_map.50 = (s32[8,16,512]{2,1,0:T(8,128)S(1)}, f32[1,128]{1,0:T(1,128)S(1)}) custom-call(f32[8,16,512]{2,1,0:T(8,128)} %ranks_hbm.1, f32[3,8,16,512]{3,2,1,0:T(8,128)} %seeds_hbm.1, s32[8,16,512]{2,1,0:T(8,128)} %flags_hbm.1), custom_call_target="tpu_custom_call" | custom-call | tf_op jit(solution)/shard_map/pallas_call | solution.py:458
  36.1 1.2 %shard_map.51 = (s32[8,16,512]{2,1,0:T(8,128)}, s32[3]{0:T(128)}) custom-call(s32[8,16,512]{2,1,0:T(8,128)S(1)} %get-tuple-element.4.state, f32[1,128]{1,0:T(1,128)S(1)} %get-tuple-element.5.totals), custom_call_target="tpu_custom_call" | custom-call | tf_op jit(solution)/shard_map/pallas_call | solution.py:466

commit v4 on v3

--- a/solution.py
+++ b/solution.py
@@ -8,6 +8,7 @@
 from jax.sharding import PartitionSpec as P
 
 ROUNDS = 3
+EARLY = 1
 MESH = pl.DeviceIdType.MESH
 UP_UP, UP_DOWN, DOWN_UP, DOWN_DOWN = (1, 1), (1, -1), (-1, 1), (-1, -1)
 DIAGONALS = (UP_UP, UP_DOWN, DOWN_UP, DOWN_DOWN)
@@ -23,8 +24,8 @@
     ranks, seeds, flags,
     bits, partial, rowmax, below, edge_y_out, edge_y_in, edge_d_out, edge_d_in,
     packed, near, near_halo, newc, row_out, row_in, diag_out, diag_in,
-    couple, whole,
-    known, load_sem, edge_send, edge_recv, round_send, round_recv, pair_send, pair_recv, all_send, all_recv,
+    couple, single, whole,
+    known, load_sem, edge_send, edge_recv, round_send, round_recv, pair_send, pair_recv, one_send, one_recv, all_send, all_recv,
 ):
     gz, gy = lax.axis_index("gz"), lax.axis_index("gy")
     depth, rows, width = ranks.shape
@@ -349,11 +350,14 @@
     outside_rowmax()
     strengths(0)
     strengths(top)
-    told(0)
-    tell(1)
 
     lane = lax.broadcasted_iota(jnp.int32, (1, 128), 1)
     counted = jnp.zeros((1, 128), jnp.float32)
+
+    def with_count(r):
+        total = jnp.sum(jnp.sum(count, axis=0, keepdims=True), axis=1, keepdims=True)
+        return jnp.where(lane == r, jnp.broadcast_to(total, counted.shape), counted)
+
     for r in range(ROUNDS):
         sent_packed = send_packed(r)
         if r == 0:
@@ -365,6 +369,10 @@
         for z in inner:
             near_inside(r, z)
         sent_rows = send_rows(r)
+        if r:
+            counted = with_count(r - 1)
+        told(r)
+        tell(r + 1)
 
         wait_all(sent_rows)
         if r == ROUNDS - 1:
@@ -385,47 +393,71 @@
         outside_z(r, False)
         count = update(r, 0, count)
         count = update(r, top, count)
-        if r < ROUNDS - 1:
-            told(r + 1)
-            tell(r + 2)
-        counted = jnp.where(lane == r, jnp.sum(count), counted)
-
-    half = ny // 2
-    lone, core = gz * half + gy // 2, lax.rem(gy, 2)
+
+    half, devices = ny // 2, nz * ny
+    column = 8 if nz % 8 == 0 else nz
+    columns, early = nz // column, EARLY if column > EARLY else 1
+    chip, core, me = gz * half + gy // 2, lax.rem(gy, 2), gz * ny + gy
+    is_early = lax.rem(gz, column) < early
+    n_early = columns * early * ny
+    counted = with_count(ROUNDS - 1)
     couple[core] = counted
     to_partner = pltpu.make_async_remote_copy(
         src_ref=couple.at[core], dst_ref=couple.at[core], send_sem=pair_send, recv_sem=pair_recv,
         device_id=(gz, gy + 1 - 2 * core), device_id_type=MESH)
     to_partner.start()
+    told(ROUNDS + 1)
+
+    def at_place(i):
+        return lax.rem(i, columns) * column + i // columns
+
+    @pl.loop(0, columns * early)
+    def _(i):
+        to_z = at_place(i)
+        for to_y in range(ny):
+            @pl.when((to_z != gz) | (to_y != gy))
+            def _():
+                pltpu.make_async_remote_copy(
+                    src_ref=couple.at[core], dst_ref=single.at[me], send_sem=one_send, recv_sem=one_recv,
+                    device_id=(to_z, to_y), device_id_type=MESH).start()
+
     to_partner.wait_recv()
-    told(ROUNDS + 1)
-    whole[lone] = couple[0] + couple[1]
-
-    def all_copy(kz, ky):
-        return pltpu.make_async_remote_copy(
-            src_ref=whole.at[lone], dst_ref=whole.at[lone], send_sem=all_send, recv_sem=all_recv,
-            device_id=(lax.rem(gz + kz, nz), lax.rem(gy + 2 * ky, ny)), device_id_type=MESH)
-
-    @pl.loop(0, nz)
+    whole[chip] = couple[0] + couple[1]
+
+    @pl.loop(columns * early, nz)
     def _(i):
-        kz = lax.rem(i + 4, nz)
-        for ky in range(1, half):
-            all_copy(kz, ky).start()
-
-        @pl.when(kz > 0)
-        def _():
-            all_copy(kz, 0).start()
-
-    others = whole.at[0 : nz * half - 1]
-    pltpu.make_async_copy(others, others, all_recv).wait()
-    totals_ref[...] = jnp.sum(whole[...], axis=0)
-    pltpu.make_async_copy(others, others, all_send).wait()
-    to_partner.wait_send()
+        to_z = at_place(i)
+        for pair in range(half):
+            @pl.when((to_z != gz) | (pair != gy // 2))
+            def _():
+                pltpu.make_async_remote_copy(
+                    src_ref=whole.at[chip], dst_ref=whole.at[chip], send_sem=all_send, recv_sem=all_recv,
+                    device_id=(to_z, 2 * pair + core), device_id_type=MESH).start()
+
+    def passed(buffer, count, sem):
+        part = buffer.at[0:count]
+        pltpu.make_async_copy(part, part, sem).wait()
 
     for (dz, dy), copy in started:
         @pl.when(there[(dz, dy)])
         def _(copy=copy):
             copy.wait_send()
+    to_partner.wait_send()
+
+    @pl.when(is_early)
+    def _():
+        single[me] = counted
+        passed(single, n_early - 1, one_send)
+        passed(whole, (devices - n_early) // 2, all_send)
+        passed(single, devices - 1, one_recv)
+        totals_ref[...] = jnp.sum(single[...], axis=0)
+
+    @pl.when(jnp.logical_not(is_early))
+    def _():
+        passed(single, n_early, one_send)
+        passed(whole, (devices - n_early) // 2 - 1, all_send)
+        passed(whole, devices // 2 - 1, all_recv)
+        totals_ref[...] = jnp.sum(whole[...], axis=0)
 
 
 def deliver(state, totals, state_out, totals_out, sem):
@@ -451,9 +483,9 @@
         vmem((depth + 2, *plane), i32),
         vmem((ROUNDS, 2, 2, depth, 1, width), f32), vmem((ROUNDS, 2, 2, depth, 1, width), f32),
         vmem((ROUNDS, 4, 2, 1, width), f32), vmem((ROUNDS, 4, 2, 1, width), f32),
-        vmem((2, 1, 128), f32), vmem((nz * ny // 2, 1, 128), f32),
+        vmem((2, 1, 128), f32), vmem((nz * ny, 1, 128), f32), vmem((nz * ny // 2, 1, 128), f32),
         pltpu.SemaphoreType.REGULAR((ROUNDS + 2,)), dma((3,)), dma((8,)), dma((8,)), dma((ROUNDS, 10)), dma((ROUNDS, 10)),
-        dma, dma, dma, dma,
+        dma, dma, dma, dma, dma, dma,
     ]
     state, totals = pl.pallas_call(
         functools.partial(kernel, nz, ny),

time: 37.5 us -> 37.1 us (0.989)
  Pallas kernels: 36.7 us -> 36.3 us
    pallas_call x1, Pallas kernels: 35.5 us -> 35.1 us  [per_device(): pl.pallas_call(functools.partial(kernel, nz, ny), out_shape=(vmem(ranks.s...]
where the time goes in v4:
time: 37.1 us; the launch traced here: 37 us
  Pallas kernels  36.3 us (98%)
  between operations  0.64 us (2%)
    pallas_call x1, Pallas kernels, per_device(): pl.pallas_call(functools.partial(kernel, nz, ny), out_shape=(vmem(ranks.s...  35.1 us
    pallas_call x1, Pallas kernels, per_device(): pl.pallas_call(deliver, out_shape=(jax.ShapeDtypeStruct(ranks.shape, i32)...  1.23 us

profile of v4, /device:TPU:1, one launch (start us, length us, event | category | flops | bytes accessed | tf_op | source)
XLA Modules:
  0.0 37.0 jit_solution(8608625840058269978)
XLA Ops:
  0.6 35.1 %shard_map.50 = (s32[8,16,512]{2,1,0:T(8,128)S(1)}, f32[1,128]{1,0:T(1,128)S(1)}) custom-call(f32[8,16,512]{2,1,0:T(8,128)} %ranks_hbm.1, f32[3,8,16,512]{3,2,1,0:T(8,128)} %seeds_hbm.1, s32[8,16,512]{2,1,0:T(8,128)} %flags_hbm.1), custom_call_target="tpu_custom_call" | custom-call | tf_op jit(solution)/shard_map/pallas_call | solution.py:490
  35.7 1.2 %shard_map.51 = (s32[8,16,512]{2,1,0:T(8,128)}, s32[3]{0:T(128)}) custom-call(s32[8,16,512]{2,1,0:T(8,128)S(1)} %get-tuple-element.4.state, f32[1,128]{1,0:T(1,128)S(1)} %get-tuple-element.5.totals), custom_call_target="tpu_custom_call" | custom-call | tf_op jit(solution)/shard_map/pallas_call | solution.py:498

commit v5 on v4

--- a/solution.py
+++ b/solution.py
@@ -460,14 +460,17 @@
         totals_ref[...] = jnp.sum(whole[...], axis=0)
 
 
-def deliver(state, totals, state_out, totals_out, sem):
-    copy = pltpu.make_async_copy(state, state_out, sem)
-    copy.start()
+def deliver(state, totals, state_out, totals_out, numbers, sems):
+    whole_state = pltpu.make_async_copy(state, state_out, sems.at[0])
+    whole_state.start()
     row = totals[...]
     lane = lax.broadcasted_iota(jnp.int32, row.shape, 1)
     for r in range(ROUNDS):
-        totals_out[r] = jnp.sum(jnp.where(lane == r, row, 0.0)).astype(jnp.int32)
-    copy.wait()
+        numbers[r] = jnp.sum(jnp.where(lane == r, row, 0.0)).astype(jnp.int32)
+    all_numbers = pltpu.make_async_copy(numbers, totals_out, sems.at[1])
+    all_numbers.start()
+    whole_state.wait()
+    all_numbers.wait()
 
 
 def per_device(nz, ny, ranks, seeds, flags):
@@ -499,8 +502,8 @@
         deliver,
         out_shape=(jax.ShapeDtypeStruct(ranks.shape, i32), jax.ShapeDtypeStruct((ROUNDS,), i32)),
         in_specs=[pl.BlockSpec(memory_space=pltpu.VMEM)] * 2,
-        out_specs=(pl.BlockSpec(memory_space=pl.ANY), pl.BlockSpec(memory_space=pltpu.SMEM)),
-        scratch_shapes=[dma],
+        out_specs=(pl.BlockSpec(memory_space=pl.ANY), pl.BlockSpec(memory_space=pl.ANY)),
+        scratch_shapes=[pltpu.SMEM((ROUNDS,), i32), dma((2,))],
     )(*[pltpu.with_memory_space_constraint(x, pltpu.VMEM) for x in (state, totals)])
 
 

time: 37.1 us -> 36.6 us (0.987)
  Pallas kernels: 36.3 us -> 35.8 us
    pallas_call x1, Pallas kernels: 1.23 us -> 0.73 us  [per_device(): pl.pallas_call(deliver, out_shape=(jax.ShapeDtypeStruct(ranks.shape, i32)...]
where the time goes in v5:
time: 36.6 us; the launch traced here: 36.5 us
  Pallas kernels  35.8 us (98%)
  between operations  0.64 us (2%)
    pallas_call x1, Pallas kernels, per_device(): pl.pallas_call(functools.partial(kernel, nz, ny), out_shape=(vmem(ranks.s...  35.1 us

profile of v5, /device:TPU:1, one launch (start us, length us, event | category | flops | bytes accessed | tf_op | source)
XLA Modules:
  0.0 36.5 jit_solution(12809471358665049158)
XLA Ops:
  0.6 35.1 %shard_map.50 = (s32[8,16,512]{2,1,0:T(8,128)S(1)}, f32[1,128]{1,0:T(1,128)S(1)}) custom-call(f32[8,16,512]{2,1,0:T(8,128)} %ranks_hbm.1, f32[3,8,16,512]{3,2,1,0:T(8,128)} %seeds_hbm.1, s32[8,16,512]{2,1,0:T(8,128)} %flags_hbm.1), custom_call_target="tpu_custom_call" | custom-call | tf_op jit(solution)/shard_map/pallas_call | solution.py:493
  35.7 0.7 %shard_map.51 = (s32[8,16,512]{2,1,0:T(8,128)}, s32[3]{0:T(128)}) custom-call(s32[8,16,512]{2,1,0:T(8,128)S(1)} %get-tuple-element.4.state, f32[1,128]{1,0:T(1,128)S(1)} %get-tuple-element.5.totals), custom_call_target="tpu_custom_call" | custom-call | tf_op jit(solution)/shard_map/pallas_call | solution.py:501

commit v6 on v5

--- a/solution.py
+++ b/solution.py
@@ -264,22 +264,23 @@
         diag_out[r, i, 0] = linked(word, LINK_Y, value)
         diag_out[r, i, 1] = linked(word, z_mask, value)
 
-    def send_packed(r):
+    def send_packed(r, low):
+        send, recv = round_send.at[r], round_recv.at[r]
+        if low:
+            return remote((-1, 0), packed.at[r, 1], packed.at[r, depth + 1], send.at[2], recv.at[2])
+        return remote((1, 0), packed.at[r, depth], packed.at[r, 0], send.at[0], recv.at[0])
+
+    def send_diag(r):
         send, recv = round_send.at[r], round_recv.at[r]
         for i, d in enumerate(DIAGONALS):
             corner(r, i, d)
-        return [
-            *[remote(d, diag_out.at[r, i], diag_in.at[r, i], send.at[6 + i], recv.at[6 + i]) for i, d in enumerate(DIAGONALS)],
-            remote((1, 0), packed.at[r, depth], packed.at[r, 0], send.at[0], recv.at[0]),
-            remote((-1, 0), packed.at[r, 1], packed.at[r, depth + 1], send.at[2], recv.at[2]),
-        ]
-
-    def send_near(r):
+        return [remote(d, diag_out.at[r, i], diag_in.at[r, i], send.at[6 + i], recv.at[6 + i]) for i, d in enumerate(DIAGONALS)]
+
+    def send_near(r, low):
         send, recv = round_send.at[r], round_recv.at[r]
-        return [
-            remote((1, 0), near.at[r, top], near_halo.at[r, 0], send.at[1], recv.at[1]),
-            remote((-1, 0), near.at[r, 0], near_halo.at[r, 1], send.at[3], recv.at[3]),
-        ]
+        if low:
+            return remote((-1, 0), near.at[r, 0], near_halo.at[r, 1], send.at[3], recv.at[3])
+        return remote((1, 0), near.at[r, top], near_halo.at[r, 0], send.at[1], recv.at[1])
 
     def send_rows(r):
         send, recv = round_send.at[r], round_recv.at[r]
@@ -358,14 +359,16 @@
         total = jnp.sum(jnp.sum(count, axis=0, keepdims=True), axis=1, keepdims=True)
         return jnp.where(lane == r, jnp.broadcast_to(total, counted.shape), counted)
 
+    packed_down, packed_up = send_packed(0, True), send_packed(0, False)
     for r in range(ROUNDS):
-        sent_packed = send_packed(r)
+        sent_diag = send_diag(r)
         if r == 0:
             strengths(1)
             strengths(top - 1)
         near_inside(r, 0)
+        near_down = send_near(r, True)
         near_inside(r, top)
-        sent_near = send_near(r)
+        near_up = send_near(r, False)
         for z in inner:
             near_inside(r, z)
         sent_rows = send_rows(r)
@@ -383,16 +386,22 @@
         count = zero
         for z in middle:
             count = update(r, z, count)
-        wait_all(sent_packed)
+        arrived(packed_up)
         finish_near(r, 0)
+        count = update(r, 1, count)
+        arrived(packed_down)
         finish_near(r, top)
-        count = update(r, 1, count)
         count = update(r, top - 1, count)
-        wait_all(sent_near)
-        outside_z(r, True)
-        outside_z(r, False)
-        count = update(r, 0, count)
-        count = update(r, top, count)
+        following = []
+        for low, z, pair, diagonals in ((True, 0, near_up, sent_diag[:2]), (False, top, near_down, sent_diag[2:])):
+            arrived(pair)
+            wait_all(diagonals)
+            outside_z(r, low)
+            count = update(r, z, count)
+            if r + 1 < ROUNDS:
+                following.append(send_packed(r + 1, low))
+        if following:
+            packed_down, packed_up = following
 
     half, devices = ny // 2, nz * ny
     column = 8 if nz % 8 == 0 else nz

time: 36.6 us -> 36.3 us (level)
  no operation moved by 1% of the time
where the time goes in v6:
time: 36.3 us; the launch traced here: 36.2 us
  Pallas kernels  35.6 us (98%)
  between operations  0.64 us (2%)
    pallas_call x1, Pallas kernels, per_device(): pl.pallas_call(functools.partial(kernel, nz, ny), out_shape=(vmem(ranks.s...  34.9 us
    pallas_call x1, Pallas kernels, per_device(): pl.pallas_call(deliver, out_shape=(jax.ShapeDtypeStruct(ranks.shape, i32)...  0.73 us

profile of v6, /device:TPU:1, one launch (start us, length us, event | category | flops | bytes accessed | tf_op | source)
XLA Modules:
  0.0 36.2 jit_solution(14765233923778024679)
XLA Ops:
  0.6 34.9 %shard_map.50 = (s32[8,16,512]{2,1,0:T(8,128)S(1)}, f32[1,128]{1,0:T(1,128)S(1)}) custom-call(f32[8,16,512]{2,1,0:T(8,128)} %ranks_hbm.1, f32[3,8,16,512]{3,2,1,0:T(8,128)} %seeds_hbm.1, s32[8,16,512]{2,1,0:T(8,128)} %flags_hbm.1), custom_call_target="tpu_custom_call" | custom-call | tf_op jit(solution)/shard_map/pallas_call | solution.py:502
  35.5 0.7 %shard_map.51 = (s32[8,16,512]{2,1,0:T(8,128)}, s32[3]{0:T(128)}) custom-call(s32[8,16,512]{2,1,0:T(8,128)S(1)} %get-tuple-element.4.state, f32[1,128]{1,0:T(1,128)S(1)} %get-tuple-element.5.totals), custom_call_target="tpu_custom_call" | custom-call | tf_op jit(solution)/shard_map/pallas_call | solution.py:510

commit v7 on v6

--- a/solution.py
+++ b/solution.py
@@ -200,11 +200,10 @@
             m = jnp.maximum(m, below[...])
         rowmax[z + 1] = m
 
-    def outside_rowmax():
-        m = partial[0]
-        rowmax[0] = jnp.maximum(m, jnp.where(first, jnp.broadcast_to(edge_d_in[0], zero.shape), 0.0))
-        m = jnp.maximum(partial[depth + 1], in_plane(top)[2])
-        rowmax[depth + 1] = jnp.maximum(m, jnp.where(first, jnp.broadcast_to(edge_d_in[3], zero.shape), 0.0))
+    def outside_rowmax(low):
+        at, i = (0, 0) if low else (depth + 1, 3)
+        m = partial[at] if low else jnp.maximum(partial[at], in_plane(top)[2])
+        rowmax[at] = jnp.maximum(m, jnp.where(first, jnp.broadcast_to(edge_d_in[i], zero.shape), 0.0))
 
     def strengths(z):
         c0, c2, c4 = in_plane(z)
@@ -344,13 +343,18 @@
         whole_rowmax(z)
     for z in middle:
         strengths(z)
-    wait_all(edge_z)
-    wait_all(edge_d)
+    whole_rowmax(top)
+    wait_all(edge_z[2:])
+    wait_all(edge_d[2:])
+    outside_rowmax(False)
+    strengths(top)
+    packed_up = send_packed(0, False)
+    wait_all(edge_z[:2])
+    wait_all(edge_d[:2])
     whole_rowmax(0)
-    whole_rowmax(top)
-    outside_rowmax()
+    outside_rowmax(True)
     strengths(0)
-    strengths(top)
+    packed_down = send_packed(0, True)
 
     lane = lax.broadcasted_iota(jnp.int32, (1, 128), 1)
     counted = jnp.zeros((1, 128), jnp.float32)
@@ -359,7 +363,6 @@
         total = jnp.sum(jnp.sum(count, axis=0, keepdims=True), axis=1, keepdims=True)
         return jnp.where(lane == r, jnp.broadcast_to(total, counted.shape), counted)
 
-    packed_down, packed_up = send_packed(0, True), send_packed(0, False)
     for r in range(ROUNDS):
         sent_diag = send_diag(r)
         if r == 0:

time: 36.3 us -> 36.4 us (level)
  no operation moved by 1% of the time
where the time goes in v7:
time: 36.4 us; the launch traced here: 36.3 us
  Pallas kernels  35.7 us (98%)
  between operations  0.64 us (2%)
    pallas_call x1, Pallas kernels, per_device(): pl.pallas_call(functools.partial(kernel, nz, ny), out_shape=(vmem(ranks.s...  35 us
    pallas_call x1, Pallas kernels, per_device(): pl.pallas_call(deliver, out_shape=(jax.ShapeDtypeStruct(ranks.shape, i32)...  0.73 us

profile of v7, /device:TPU:1, one launch (start us, length us, event | category | flops | bytes accessed | tf_op | source)
XLA Modules:
  0.0 36.3 jit_solution(14943531379606778127)
XLA Ops:
  0.6 35.0 %shard_map.50 = (s32[8,16,512]{2,1,0:T(8,128)S(1)}, f32[1,128]{1,0:T(1,128)S(1)}) custom-call(f32[8,16,512]{2,1,0:T(8,128)} %ranks_hbm.1, f32[3,8,16,512]{3,2,1,0:T(8,128)} %seeds_hbm.1, s32[8,16,512]{2,1,0:T(8,128)} %flags_hbm.1), custom_call_target="tpu_custom_call" | custom-call | tf_op jit(solution)/shard_map/pallas_call | solution.py:505
  35.6 0.7 %shard_map.51 = (s32[8,16,512]{2,1,0:T(8,128)}, s32[3]{0:T(128)}) custom-call(s32[8,16,512]{2,1,0:T(8,128)S(1)} %get-tuple-element.4.state, f32[1,128]{1,0:T(1,128)S(1)} %get-tuple-element.5.totals), custom_call_target="tpu_custom_call" | custom-call | tf_op jit(solution)/shard_map/pallas_call | solution.py:513
